TPU v7x, 128 devices: a whole 4x4x4 slice. The times are simulated.
128 devices in a mesh: graph: 128 (over z, y, x, core).
Axes of the slice: x: 4, y: 4, z: 4, core: 2. Of those that a mesh axis runs over, the one named last changes fastest.
Arguments:
- node_feats: bfloat16 [131072, 1024], P('graph')
- w_one: float32 [1024, 128], replicated
- w_two: float32 [128, 19], replicated
- send_idx: int32 [256, 512], P('graph')
- edge_src: int32 [2097152], P('graph')
- edge_dst: int32 [2097152], P('graph')
- edge_w: float32 [2097152], P('graph')
- labels: int32 [131072], P('graph')
- label_mask: int32 [131072], P('graph')
Outputs:
- output 1: float32 [], replicated
- output 2: float32 [1024, 128], replicated
- output 3: float32 [128, 19], replicated
All inputs are finite; a program needn't handle non-finite values.
Results may differ from a plain program's by a relative error of at most 0.001.
Values are sent between devices in bfloat16 or wider.
A program may use at most 1 GiB of HBM per device.

v0:
```python
import jax
import jax.numpy as jnp
from jax import lax
from jax.sharding import PartitionSpec as P

GRAPH_AXIS = "graph"
CONTRACT_ROWS = (((0,), (0,)), ((), ()))
CONTRACT_COLS = (((1,), (1,)), ((), ()))


def solution(mesh):
    num_dev = mesh.shape[GRAPH_AXIS]
    to_next = [(dev_id, (dev_id + 1) % num_dev) for dev_id in range(num_dev)]
    to_prev = [(dev_id, (dev_id - 1) % num_dev) for dev_id in range(num_dev)]

    def halo_extend(node_table, send_rows):
        from_prev = lax.ppermute(node_table[send_rows[1]], GRAPH_AXIS, to_next)
        from_next = lax.ppermute(node_table[send_rows[0]], GRAPH_AXIS, to_prev)
        return jnp.concatenate([node_table, from_prev, from_next], axis=0)

    def aggregate(ext_table, edge_src, edge_dst, edge_w, rows_loc):
        return jax.ops.segment_sum(edge_w[:, None] * ext_table[edge_src], edge_dst, num_segments=rows_loc)

    def scatter_back(grad_rows, send_rows, edge_src, edge_dst, edge_w):
        rows_loc = grad_rows.shape[0]
        halo_rows = send_rows.shape[1]
        ext_grad = jax.ops.segment_sum(edge_w[:, None] * grad_rows[edge_dst], edge_src, num_segments=rows_loc + 2 * halo_rows)
        back_prev = lax.ppermute(ext_grad[rows_loc:rows_loc + halo_rows], GRAPH_AXIS, to_prev)
        back_next = lax.ppermute(ext_grad[rows_loc + halo_rows:], GRAPH_AXIS, to_next)
        row_ids = jnp.concatenate([send_rows[1], send_rows[0]])
        return ext_grad[:rows_loc].at[row_ids].add(jnp.concatenate([back_prev, back_next], axis=0))

    def device_step(node_feats, w_one, w_two, send_rows, edge_src, edge_dst, edge_w, labels, label_mask):
        rows_loc = node_feats.shape[0]
        w_one_b = w_one.astype(jnp.bfloat16)
        w_two_b = w_two.astype(jnp.bfloat16)
        tab_one = jnp.dot(node_feats, w_one_b, preferred_element_type=jnp.float32).astype(jnp.bfloat16)
        pre_one = aggregate(halo_extend(tab_one, send_rows), edge_src, edge_dst, edge_w, rows_loc)
        hidden = jnp.maximum(pre_one, 0.0).astype(jnp.bfloat16)
        tab_two = jnp.dot(hidden, w_two_b, preferred_element_type=jnp.float32).astype(jnp.bfloat16)
        logits = aggregate(halo_extend(tab_two, send_rows), edge_src, edge_dst, edge_w, rows_loc)
        mask_f = label_mask.astype(jnp.float32)
        label_count = jnp.maximum(lax.psum(jnp.sum(mask_f), GRAPH_AXIS), 1.0)
        log_norm = jax.nn.logsumexp(logits, axis=1)
        one_hot = (labels[:, None] == jnp.arange(logits.shape[1])[None, :]).astype(jnp.float32)
        picked = jnp.sum(logits * one_hot, axis=1)
        mean_loss = lax.psum(jnp.sum(mask_f * (log_norm - picked)), GRAPH_AXIS) / label_count
        d_logits = (jnp.exp(logits - log_norm[:, None]) - one_hot) * (mask_f / label_count)[:, None]
        d_tab_two = scatter_back(d_logits, send_rows, edge_src, edge_dst, edge_w).astype(jnp.bfloat16)
        grad_two = lax.psum(lax.dot_general(hidden, d_tab_two, CONTRACT_ROWS, preferred_element_type=jnp.float32), GRAPH_AXIS)
        d_hidden = lax.dot_general(d_tab_two, w_two_b, CONTRACT_COLS, preferred_element_type=jnp.float32)
        d_pre = jnp.where(pre_one > 0.0, d_hidden, 0.0)
        d_tab_one = scatter_back(d_pre, send_rows, edge_src, edge_dst, edge_w).astype(jnp.bfloat16)
        grad_one = lax.psum(lax.dot_general(node_feats, d_tab_one, CONTRACT_ROWS, preferred_element_type=jnp.float32), GRAPH_AXIS)
        return mean_loss, grad_one, grad_two

    row_spec = P(GRAPH_AXIS)
    return jax.shard_map(device_step, mesh=mesh, in_specs=(row_spec, P(), P(), row_spec, row_spec, row_spec, row_spec, row_spec, row_spec), out_specs=(P(), P(), P()), check_vma=False)
```

profile of v0, /device:TPU:1, one launch (start us, length us, event | category | flops | bytes accessed | tf_op | source)
XLA Modules:
  0.0 1026.4 jit_solution(9225709569704249322)
XLA Ops:
  7.2 0.0 copy-start
  7.2 0.0 all-reduce.3.cloned.1.call-start
  7.2 0.9 compare_select_fusion.5
  8.1 0.7 copy-done
  8.8 1.8 convolution_convert_fusion
  10.6 0.0 copy-start.1
  10.6 1.3 gather_fusion
  11.9 0.0 copy-start.5
  12.0 2.7 collective-permute-start
  14.6 1.3 gather_fusion.1
  16.0 0.0 copy-done.7
  16.0 0.1 collective-permute-start.1
  16.1 0.0 copy-done.4
  16.1 0.0 copy-done.3
  16.1 0.4 collective-permute-done
  16.6 3.9 collective-permute-done.1
  20.5 0.0 copy-done.1
  20.5 0.0 copy-start.8
  20.5 145.0 %scatter_custom_fusion = f32[1024,128]{1,0:T(8,128)S(1)} fusion(s32[16384]{0:T(1024)S(1)} %copy-done.3, f32[16384]{0:T(1024)S(1)} %copy-done.1, f32[]{:T(128)} %constant.6.clone.1, bf16[2048,128]{1,0:T(8,128)(2,1)S(1)} %pad_maximum_fusion, s32[16384]{0:T(1024)S(1)} %fusion.34), kind=kCustom, calls=%fused_computation.21 | custom fusion | flops 6291456 | bytes 1179652 | tf_op jit(solution)/shard_map/scatter-add | solution.py:22
  165.6 0.2 convolution_convert_fusion.1
  165.8 0.2 copy.39
  166.0 1.5 gather_fusion.3
  167.5 0.0 copy-start.6
  167.5 1.3 gather_fusion.2
  168.9 0.0 copy-start.9
  168.9 0.1 copy.40
  169.0 0.1 copy.42
  169.1 5.3 collective-permute-start.3
  174.3 0.0 collective-permute-start.2
  174.3 0.0 copy-done.8
  174.3 0.6 slice_bitcast_fusion.1
  174.9 0.2 collective-permute-done.3
  175.2 7.1 collective-permute-done.2
  182.3 1.0 copy.43
  183.4 189.9 %scatter_custom_fusion.1 = f32[1024,19]{1,0:T(8,128)S(1)} fusion(s32[16384]{0:T(1024)S(1)} %copy-done.3, f32[16384]{0:T(1024)S(1)} %copy-done.1, f32[]{:T(128)} %constant.6.clone.1, bf16[2048,19]{1,0:T(8,128)(2,1)} %copy.43, s32[16384]{0:T(1024)S(1)} %fusion.34), kind=kCustom, calls=%fused_computation.18 | custom fusion | flops 933888 | bytes 286724 | tf_op jit(solution)/shard_map/scatter-add | solution.py:22
  373.3 0.2 reduce_max.9
  373.5 0.6 select_reduce_fusion
  374.1 0.6 convert_reduce_fusion
  374.8 69.4 %psum.29 = f32[]{:T(128)} all-reduce(f32[]{:T(128)} %get-tuple-element.20), channel_id=1, replica_groups=mesh['graph'=128] {'graph'}, use_global_device_ids=true, to_apply=%region_8.0 | all-reduce | flops 1 | bytes 8 | tf_op jit(solution)/shard_map/psum | solution.py:43
  444.8 1.3 subtract_multiply_fusion
  446.1 191.6 %scatter_custom_fusion.2 = f32[2048,19]{1,0:T(8,128)} fusion(s32[16384]{0:T(1024)} %param.13, f32[16384]{0:T(1024)S(1)} %copy-done.1, f32[]{:T(128)} %constant.6.clone.1, f32[1024,19]{1,0:T(8,128)} %subtract_multiply_fusion, s32[16384]{0:T(1024)S(1)} %fusion.35), kind=kCustom, calls=%fused_computation.16 | custom fusion | flops 622592 | bytes 811520 | tf_op jit(solution)/shard_map/scatter-add | solution.py:27
  637.7 1.1 fusion.45
  638.8 1.2 collective-permute-start.4
  640.0 0.7 collective-permute-start.5
  640.6 0.7 compare_select_fusion.3
  641.3 3.4 collective-permute-done.4
  644.7 0.0 collective-permute-done.5
  644.7 0.7 copy-done.2
  645.4 6.7 scatter_custom_fusion.3
  652.1 1.0 compare_select_fusion
  653.1 191.6 %scatter_custom_fusion.4 = f32[2048,128]{1,0:T(8,128)} fusion(s32[16384]{0:T(1024)} %param.13, f32[16384]{0:T(1024)S(1)} %copy-done.1, f32[]{:T(128)} %constant.6.clone.1, f32[1024,128]{1,0:T(8,128)} %compare_select_fusion, s32[16384]{0:T(1024)S(1)} %fusion.35), kind=kCustom, calls=%fused_computation.14 | custom fusion | flops 4194304 | bytes 1704448 | tf_op jit(solution)/shard_map/scatter-add | solution.py:27
  844.6 1.1 fusion.44
  845.7 8.2 collective-permute-start.6
  853.8 0.0 collective-permute-start.7
  853.8 1.9 slice.57
  855.7 0.0 collective-permute-done.6
  855.7 1.4 collective-permute-done.7
  857.1 7.5 scatter_custom_fusion.5
  864.6 2.3 convolution_bitcast_fusion
  866.9 0.0 all-reduce.3.cloned.1.call-update
  867.0 0.2 fusion.28
  867.2 69.8 %all-reduce = (f32[]{:T(128)}, f32[128,19]{0,1:T(8,128)}) all-reduce(f32[]{:T(128)} %get-tuple-element.21, f32[128,19]{0,1:T(8,128)S(1)} %fusion.28), channel_id=1, replica_groups=mesh['graph'=128] {'graph'}, use_global_device_ids=true, to_apply=%region_6.0 | all-reduce | flops 2433 | bytes 19464 | tf_op jit(solution)/shard_map/psum | solution.py:47
  937.6 78.8 %all-reduce.3.cloned.1.call-done = f32[1024,128]{0,1:T(8,128)} async-done(((f32[1024,128]{0,1:T(8,128)}), f32[1024,128]{0,1:T(8,128)}) %all-reduce.3.cloned.1.call-update) | async-done | bytes 524304 | tf_op jit(solution)/shard_map/psum | solution.py:54
  1016.4 2.0 copy.44
  (17 shorter events, 0.1 us)
Async XLA Ops:
  7.2 1.6 copy-start
  7.2 1009.2 %all-reduce.3.cloned.1.call-start = ((), (), s32[]{:S(2)}) async-start(), calls=%async_computation | async-start | bytes 1048576 | tf_op jit(solution)/shard_map/psum | solution.py:54
  8.8 7.3 copy-start.4
  8.8 7.3 copy-start.3
  10.6 9.9 copy-start.1
  11.9 153.6 %copy-start.5 = (f32[128,19]{0,1:T(8,128)S(1)}, f32[128,19]{0,1:T(8,128)}, u32[]{:S(2)}) copy-start(f32[128,19]{0,1:T(8,128)} %param.11) | copy-start | bytes 29188
  12.0 4.6 collective-permute-start
  14.6 1.3 copy-start.7
  16.0 4.5 collective-permute-start.1
  20.5 153.9 %copy-start.8 = (s32[2,512]{1,0:T(2,128)S(1)}, s32[2,512]{1,0:T(2,128)}, u32[]{:S(2)}) copy-start(s32[2,512]{1,0:T(2,128)} %param.12) | copy-start | bytes 12292
  167.5 206.0 %copy-start.6 = (s32[1024]{0:T(1024)S(1)}, s32[1024]{0:T(1024)}, u32[]{:S(2)}) copy-start(s32[1024]{0:T(1024)} %param.16) | copy-start | bytes 12292
  168.9 205.3 %copy-start.9 = (s32[1024]{0:T(1024)S(1)}, s32[1024]{0:T(1024)}, u32[]{:S(2)}) copy-start(s32[1024]{0:T(1024)} %param.17) | copy-start | bytes 12292
  169.1 6.1 collective-permute-start.3
  174.3 8.0 collective-permute-start.2
  637.7 7.7 slice-start
  638.8 5.9 collective-permute-start.4
  640.0 4.7 collective-permute-start.5
  644.7 0.7 copy-start.2
  845.7 10.0 collective-permute-start.6
  853.8 3.3 collective-permute-start.7
Sparse Core Ops, SparseCore 0:
  867.1 149.2 all-reduce.2
where the time goes:
time: 1030 us
  other arithmetic  737 us (72%)
  blocking collectives  139 us (13%)
  waiting for transfers between devices  95.3 us (9%)
  starting transfers between devices  18 us (2%)
  between operations  16.7 us (2%)
  local copies, waits for them, and re-layouts  15.1 us (1%)
    scatter-add x2, other arithmetic, scatter_back(): jax.ops.segment_sum(edge_w[:, None] * grad_rows[edge_dst], edge_src, num_...  383 us
    scatter-add x2, other arithmetic, aggregate(): jax.ops.segment_sum(edge_w[:, None] * ext_table[edge_src], edge_dst, num_...  335 us
    psum x1, waiting for transfers between devices, device_step(): lax.psum(lax.dot_general(node_feats, d_tab_one, CONTRACT_ROWS, preferred_...  78.8 us
    psum x1, blocking collectives, device_step(): lax.psum(jnp.sum(mask_f * (log_norm - picked)), GRAPH_AXIS) / label_count  69.8 us
    psum x1, blocking collectives, device_step(): label_count = jnp.maximum(lax.psum(jnp.sum(mask_f), GRAPH_AXIS), 1.0)  69.4 us
  transfers between devices with their start and end apart: 9, of which 7 were waited for; matrix products, arithmetic and copies ran while one was open for 0% of the time, Pallas kernels for 0%

commit v1 on v0

v1 whole, which is shorter than its diff:
```python
import functools

import jax
import jax.numpy as jnp
from jax import lax
from jax.experimental import pallas as pl
from jax.experimental.pallas import tpu as pltpu
from jax.sharding import PartitionSpec as P

AXIS = "graph"
F32 = jnp.float32
BF16 = jnp.bfloat16
NODES = 1024
HALO = 512
EXT = NODES + 2 * HALO
HID = 128
PADC = 32
BATCH = 128
GROUP = 16
NB = 4
ROW_N = (((1,), (0,)), ((), ()))
ROW_T = (((1,), (1,)), ((), ()))


def split3(x):
    high = x.astype(BF16)
    rest = x - high.astype(F32)
    mid = rest.astype(BF16)
    low = (rest - mid.astype(F32)).astype(BF16)
    return high, mid, low


def dot_n(a, b):
    return lax.dot_general(a, b, ROW_N, preferred_element_type=F32)


def dot_t(a, b):
    return lax.dot_general(a, b, ROW_T, preferred_element_type=F32)


def build_kernel(src_ref, dst_ref, w_ref, bh_ref, bm_ref, bl_ref, m_ref, rs0, rs1, row_v, wh, wm, wl, *rest):
    us0, us1, sem = rest[:NB], rest[NB:2 * NB], rest[2 * NB]
    n_batch = src_ref.shape[0]
    row_v[...] = ((dst_ref[...] >> 7) << 11) + src_ref[...]
    h, m, l = split3(w_ref[...])
    wh[...] = h.astype(F32)
    wm[...] = m.astype(F32)
    wl[...] = l.astype(F32)
    n_half = n_batch // NB

    def rows_copy(i, rs, k):
        return pltpu.make_async_copy(row_v.at[pl.ds(pl.multiple_of(i * NB, NB), NB), :], rs, sem.at[k])

    rows_copy(0, rs0, 0).start()

    def zero(i, c):
        m_ref[pl.ds(pl.multiple_of(i * 256, 256), 256), :] = jnp.zeros((256, 128), F32)
        return c

    lax.fori_loop(0, m_ref.shape[0] // 256, zero, 0)
    ii = lax.broadcasted_iota(jnp.int32, (BATCH, BATCH), 1)
    jj = lax.broadcasted_iota(jnp.int32, (BATCH, BATCH), 0)
    tri = jnp.logical_and(ii <= jj, (ii >> 4) == (jj >> 4))

    def make_u(b, u):
        rb = jnp.broadcast_to(row_v[pl.ds(b, 1), :], (BATCH, BATCH))
        same = jnp.where(jnp.logical_and(rb == rb.T, tri), 1.0, 0.0).astype(BF16)
        hit = jj == (dst_ref[pl.ds(b, 1), :] & 127)
        acc = None
        for piece in (wh, wm, wl):
            v = jnp.where(hit, piece[pl.ds(b, 1), :], 0.0).astype(BF16)
            d = dot_t(same, v)
            acc = d if acc is None else acc + d
        u[...] = acc

    def rmw(k, rs, u):
        for g in range(BATCH // GROUP):
            rows = [rs[k, g * GROUP + j] for j in range(GROUP)]
            vals = [m_ref[pl.ds(rows[j], 1), :] + u[pl.ds(g * GROUP + j, 1), :] for j in range(GROUP)]
            for j in range(GROUP):
                m_ref[pl.ds(rows[j], 1), :] = vals[j]

    for k in range(NB):
        make_u(k, us0[k])

    def body(t, c):
        b = 2 * NB * t
        rows_copy(2 * t, rs0, 0).wait()
        rows_copy(2 * t + 1, rs1, 1).start()
        for k in range(NB):
            make_u(b + NB + k, us1[k])
        for k in range(NB):
            rmw(k, rs0, us0[k])
        rows_copy(2 * t + 1, rs1, 1).wait()
        nxt = jnp.minimum(2 * t + 2, n_half - 1)
        rows_copy(nxt, rs0, 0).start()
        for k in range(NB):
            make_u(nxt * NB + k, us0[k])
        for k in range(NB):
            rmw(k, rs1, us1[k])
        return c

    lax.fori_loop(0, n_half // 2, body, 0)
    rows_copy(n_half - 1, rs0, 0).wait()

    def out(i, c):
        rows = pl.ds(pl.multiple_of(i * 128, 128), 128)
        for j in range(NODES // 128):
            h, m, l = split3(m_ref[pl.ds(pl.multiple_of(j * EXT + i * 128, 128), 128), :])
            cols = pl.ds(j * 128, 128)
            bh_ref[rows, cols] = h
            bm_ref[rows, cols] = m
            bl_ref[rows, cols] = l
        return c

    lax.fori_loop(0, EXT // 128, out, 0)


def build(src, dst, w):
    n = src.shape[0]
    nb = n // BATCH
    piece = jax.ShapeDtypeStruct((EXT, NODES), BF16)
    vmem = pl.BlockSpec(memory_space=pltpu.VMEM)
    return pl.pallas_call(
        build_kernel,
        out_shape=[piece] * 3,
        in_specs=[vmem] * 3,
        out_specs=[vmem] * 3,
        scratch_shapes=[
            pltpu.VMEM((8 * EXT, 128), F32),
            pltpu.SMEM((NB, BATCH), jnp.int32),
            pltpu.SMEM((NB, BATCH), jnp.int32),
            pltpu.VMEM((nb, BATCH), jnp.int32),
        ]
        + [pltpu.VMEM((nb, BATCH), F32)] * 3
        + [pltpu.VMEM((BATCH, 128), F32)] * (2 * NB)
        + [pltpu.SemaphoreType.DMA((2,))],
        name="build",
        compiler_params=pltpu.CompilerParams(vmem_limit_bytes=40 * 1024 * 1024),
    )(src.reshape(nb, BATCH), dst.reshape(nb, BATCH), w.reshape(nb, BATCH))


def step_kernel(
    x_ref, w1_ref, w2t_ref, w2_ref, send_ref, bh_ref, bm_ref, bl_ref, lab_ref, mask_ref,
    loss_ref, out_ref, two_ref,
    s0_ref, s1_ref, sb1, hp1, hn1, sb2, hp2, hn2, gb2, ra2, rb2, gb1, ra1, rb1,
    y_ref, hid_ref, part, rc, a1, rx, a2, ry, a3, rz, cnt, cntr, sml, smlr, own_ref, dy_ref, ssem, rsem,
):
    me = lax.axis_index(AXIS)
    num = 128
    core = lax.rem(me, 2)
    cx = lax.rem(me // 2, 4)
    cy = lax.rem(me // 8, 4)
    cz = me // 32
    nxt = lax.rem(me + 1, num)
    prv = lax.rem(me + num - 1, num)
    twin = me + 1 - 2 * core
    dims = ((cx, 2), (cy, 8), (cz, 32))

    def peer(dim, d):
        c, stride = dims[dim]
        p = lax.rem(c + d, 4)
        return p, me + (p - c) * stride

    barrier = pltpu.get_barrier_semaphore()
    targets = [nxt, prv, twin] + [peer(k, d)[1] for k in range(3) for d in (1, 2, 3)]
    for t in targets:
        pl.semaphore_signal(barrier, inc=1, device_id=(t,), device_id_type=pl.DeviceIdType.MESH)
    pl.semaphore_wait(barrier, len(targets))

    counter = [0]

    def copy(src, dst, dev):
        k = counter[0]
        counter[0] += 1
        c = pltpu.make_async_remote_copy(
            src_ref=src, dst_ref=dst, send_sem=ssem.at[k], recv_sem=rsem.at[k],
            device_id=(dev,), device_id_type=pl.DeviceIdType.MESH,
        )
        c.start()
        return c

    cnt[...] = jnp.broadcast_to(jnp.sum(mask_ref[...].astype(F32), axis=1, keepdims=True), (8, 128))

    def small_start(val, recv, stage):
        if stage == 0:
            return [copy(val, recv.at[0, 0], twin)]
        c, _ = dims[stage - 1]
        recv[stage, c] = val[...]
        return [copy(val, recv.at[stage, c], peer(stage - 1, d)[1]) for d in (1, 2, 3)]

    def small_end(copies, val, recv, stage):
        for c in copies:
            c.wait()
        if stage == 0:
            val[...] = val[...] + recv[0, 0]
        else:
            val[...] = (recv[stage, 0] + recv[stage, 1]) + (recv[stage, 2] + recv[stage, 3])

    cc = small_start(cnt, cntr, 0)

    node = lax.broadcasted_iota(jnp.int32, (NODES, HALO), 0)
    s0_ref[...] = jnp.where(node == send_ref[0:1, :], 1.0, 0.0).astype(BF16)
    s1_ref[...] = jnp.where(node == send_ref[1:2, :], 1.0, 0.0).astype(BF16)

    t1 = dot_n(x_ref[...], w1_ref[...].astype(BF16))
    t1 = t1.T.astype(BF16)
    sb1[1] = dot_n(t1, s1_ref[...]).astype(BF16)
    sb1[0] = dot_n(t1, s0_ref[...]).astype(BF16)
    c_p = copy(sb1.at[1], hp1, nxt)
    c_n = copy(sb1.at[0], hn1, prv)

    def agg(e, lo, hi):
        acc = dot_n(e, bl_ref[lo:hi, :])
        acc = acc + dot_n(e, bm_ref[lo:hi, :])
        return acc + dot_n(e, bh_ref[lo:hi, :])

    y_ref[...] = agg(t1, 0, NODES)
    small_end(cc, cnt, cntr, 0)
    cc = small_start(cnt, cntr, 1)
    c_p.wait()
    c_n.wait()
    y = y_ref[...] + (agg(hp1[...], NODES, NODES + HALO) + agg(hn1[...], NODES + HALO, EXT))
    y_ref[...] = y
    small_end(cc, cnt, cntr, 1)
    cc = small_start(cnt, cntr, 2)
    hid = jnp.maximum(y, 0.0).astype(BF16)
    hid_ref[...] = hid
    t2 = dot_n(w2t_ref[...], hid).astype(BF16)
    sb2[1] = dot_n(t2, s1_ref[...]).astype(BF16)
    sb2[0] = dot_n(t2, s0_ref[...]).astype(BF16)
    c_p = copy(sb2.at[1], hp2, nxt)
    c_n = copy(sb2.at[0], hn2, prv)
    z = agg(t2, 0, NODES)
    small_end(cc, cnt, cntr, 2)
    cc = small_start(cnt, cntr, 3)
    c_p.wait()
    c_n.wait()
    z = z + (agg(hp2[...], NODES, NODES + HALO) + agg(hn2[...], NODES + HALO, EXT))
    small_end(cc, cnt, cntr, 3)
    count = jnp.maximum(cnt[0:1, 0:1], 1.0)

    cls = lax.broadcasted_iota(jnp.int32, (PADC, NODES), 0)
    real = cls < 19
    mask = mask_ref[...].astype(F32)
    zm = jnp.where(real, z, -jnp.inf)
    top = jnp.max(zm, axis=0, keepdims=True)
    norm = jnp.log(jnp.sum(jnp.where(real, jnp.exp(z - top), 0.0), axis=0, keepdims=True)) + top
    hot = (cls == lab_ref[...]).astype(F32)
    picked = jnp.sum(z * hot, axis=0, keepdims=True)
    loss = jnp.sum(mask * (norm - picked), axis=1, keepdims=True)
    dz = (jnp.where(real, jnp.exp(z - norm), 0.0) - hot) * (mask / count)

    def agg_back(d, lo, hi):
        n = d.shape[0]
        dh, dm, dl = split3(d)
        rh = dot_t(jnp.concatenate([dh, dm, dl], axis=0), bh_ref[lo:hi, :])
        rm = dot_t(jnp.concatenate([dh, dm], axis=0), bm_ref[lo:hi, :])
        rl = dot_t(dh, bl_ref[lo:hi, :])
        return rh[0:n] + ((rh[n:2 * n] + rm[0:n]) + (rh[2 * n:3 * n] + (rm[n:2 * n] + rl)))

    def returned(r, s_ref):
        n = r.shape[0]
        t = dot_t(jnp.concatenate(split3(r), axis=0), s_ref[...])
        return t[0:n] + (t[n:2 * n] + t[2 * n:3 * n])

    gb2[0] = agg_back(dz, NODES, NODES + HALO)
    c_p = copy(gb2.at[0], ra2, prv)
    gb2[1] = agg_back(dz, NODES + HALO, EXT)
    c_n = copy(gb2.at[1], rb2, nxt)
    own = agg_back(dz, 0, NODES)
    c_p.wait()
    c_n.wait()
    dt2 = (own + (returned(ra2[...], s1_ref) + returned(rb2[...], s0_ref))).astype(BF16)
    g2 = dot_t(dt2, hid_ref[...])
    sml[...] = g2
    sml[24:32, :] = jnp.broadcast_to(loss, (8, 128))
    cs = small_start(sml, smlr, 0)
    dh = dot_n(w2_ref[...], dt2)
    dy_ref[...] = jnp.where(y_ref[...] > 0.0, dh, 0.0)
    gb1[0] = agg_back(dy_ref[...], NODES, NODES + HALO)
    c_p = copy(gb1.at[0], ra1, prv)
    gb1[1] = agg_back(dy_ref[...], NODES + HALO, EXT)
    c_n = copy(gb1.at[1], rb1, nxt)
    small_end(cs, sml, smlr, 0)
    cs = small_start(sml, smlr, 1)
    own_ref[...] = agg_back(dy_ref[...], 0, NODES)
    small_end(cs, sml, smlr, 1)
    cs = small_start(sml, smlr, 2)
    c_p.wait()
    c_n.wait()
    dt1 = (own_ref[...] + (returned(ra1[...], s1_ref) + returned(rb1[...], s0_ref))).astype(BF16)
    small_end(cs, sml, smlr, 2)
    cs = small_start(sml, smlr, 3)
    part[...] = dot_n(dt1, x_ref[...]).T

    mine = pl.ds(pl.multiple_of(core * 512, 512), 512)
    other = pl.ds(pl.multiple_of((1 - core) * 512, 512), 512)
    copy(part.at[other], rc, twin).wait()
    a1[...] = part[mine, :] + rc[...]

    def scatter_stage(dim, val, recv, size, res):
        c, _ = dims[dim]
        cps = []
        for d in (1, 2, 3):
            p, dev = peer(dim, d)
            cps.append(copy(val.at[pl.ds(pl.multiple_of(p * size, size), size)], recv.at[d - 1], dev))
        for k in cps:
            k.wait()
        res[...] = (val[pl.ds(pl.multiple_of(c * size, size), size), :] + recv[0]) + (recv[1] + recv[2])

    scatter_stage(0, a1, rx, 128, a2)
    small_end(cs, sml, smlr, 3)
    scatter_stage(1, a2, ry, 32, a3)
    spot = core * 512 + cx * 128 + cy * 32 + cz * 8
    scatter_stage(2, a3, rz, 8, out_ref.at[pl.ds(pl.multiple_of(spot, 8), 8)])

    def gather_stage(dim, start, size):
        rows = out_ref.at[pl.ds(pl.multiple_of(start, size), size)]
        cps = [copy(rows, rows, peer(dim, d)[1]) for d in (1, 2, 3)]
        for k in cps:
            k.wait()

    gather_stage(2, spot, 8)
    gather_stage(1, core * 512 + cx * 128 + cy * 32, 32)
    gather_stage(0, core * 512 + cx * 128, 128)
    half = out_ref.at[mine]
    last = copy(half, half, twin)
    loss_ref[...] = sml[24:25, 0:1] / count
    two_ref[...] = sml[...].T[:, 0:19]
    last.wait()


def step(x, w_one, w_two, send_rows, src, dst, w, labels, mask):
    bh, bm, bl = build(src, dst, w)
    w2 = w_two.astype(BF16)
    w2t = jnp.zeros((PADC, HID), BF16).at[:19, :].set(w2.T)
    w2p = jnp.zeros((HID, PADC), BF16).at[:, :19].set(w2)
    vmem = pl.BlockSpec(memory_space=pltpu.VMEM)
    n_sem = 10 + 4 + 4 + 10 + 20
    V = pltpu.VMEM
    loss, one, two = pl.pallas_call(
        step_kernel,
        out_shape=[
            jax.ShapeDtypeStruct((1, 1), F32),
            jax.ShapeDtypeStruct((1024, HID), F32),
            jax.ShapeDtypeStruct((HID, 19), F32),
        ],
        in_specs=[vmem] * 10,
        out_specs=[vmem] * 3,
        scratch_shapes=[
            V((NODES, HALO), BF16), V((NODES, HALO), BF16),
            V((2, HID, HALO), BF16), V((HID, HALO), BF16), V((HID, HALO), BF16),
            V((2, PADC, HALO), BF16), V((PADC, HALO), BF16), V((PADC, HALO), BF16),
            V((2, PADC, HALO), F32), V((PADC, HALO), F32), V((PADC, HALO), F32),
            V((2, HID, HALO), F32), V((HID, HALO), F32), V((HID, HALO), F32),
            V((HID, NODES), F32), V((HID, NODES), BF16),
            V((1024, HID), F32), V((512, HID), F32), V((512, HID), F32),
            V((3, 128, HID), F32), V((128, HID), F32), V((3, 32, HID), F32), V((32, HID), F32), V((3, 8, HID), F32),
            V((8, 128), F32), V((4, 4, 8, 128), F32), V((PADC, 128), F32), V((4, 4, PADC, 128), F32),
            V((HID, NODES), F32), V((HID, NODES), F32),
            pltpu.SemaphoreType.DMA((n_sem,)), pltpu.SemaphoreType.DMA((n_sem,)),
        ],
        name="step",
        compiler_params=pltpu.CompilerParams(
            collective_id=0, has_side_effects=True, vmem_limit_bytes=56 * 1024 * 1024
        ),
    )(x, w_one, w2t, w2p, send_rows, bh, bm, bl, labels.reshape(1, NODES), mask.reshape(1, NODES))
    return loss.reshape(()), one, two


def solution(mesh):
    row = P(AXIS)
    return jax.shard_map(
        step, mesh=mesh, in_specs=(row, P(), P(), row, row, row, row, row, row),
        out_specs=(P(), P(), P()), check_vma=False,
    )
```

time: 1030 us -> 139 us (0.13)
  other arithmetic: 737 us -> 1.29 us
  blocking collectives: 139 us -> 0 us
  Pallas kernels: 0 us -> 121 us
  waiting for transfers between devices: 95.3 us -> 0 us
  starting transfers between devices: 18 us -> 0 us
  between operations: 16.7 us -> 2.41 us
    scatter-add x6 -> x0, other arithmetic: 732 us -> none  [the longest x2 383 us: scatter_back(): jax.ops.segment_sum(edge_w[:, None] * grad_rows[edge_dst], edge_src, num_...]
    psum x2 -> x0, blocking collectives: 139 us -> none  [the longest x1 69.8 us: device_step(): lax.psum(jnp.sum(mask_f * (log_norm - picked)), GRAPH_AXIS) / label_count]
    pallas_call x0 -> x2, Pallas kernels: none -> 121 us  [the longest x1 84.7 us: step(): pl.pallas_call(step_kernel, out_shape=[jax.ShapeDtypeStruct((1, 1), F32),...]
    psum x1 -> x0, waiting for transfers between devices: 78.8 us -> none  [device_step(): lax.psum(lax.dot_general(node_feats, d_tab_one, CONTRACT_ROWS, preferred_...]
    ppermute x8 -> x0, starting transfers between devices: 18 us -> none  [the longest x2 9.32 us: scatter_back(): lax.ppermute(ext_grad[rows_loc:rows_loc + halo_rows], GRAPH_AXIS, to_prev)]
    ppermute x8 -> x0, waiting for transfers between devices: 16.5 us -> none  [the longest x2 7.57 us: halo_extend(): from_prev = lax.ppermute(node_table[send_rows[1]], GRAPH_AXIS, to_next)]
  transfers between devices with their start and end apart: 9 -> 0, of which waited for: 7 -> 0; matrix products, arithmetic and copies ran while one was open for 0% -> 0% of each run, Pallas kernels for 0% -> 0%
where the time goes in v1:
time: 139 us
  Pallas kernels  121 us (87%)
  local copies, waits for them, and re-layouts  13.9 us (10%)
  between operations  2.41 us (2%)
    pallas_call x1, Pallas kernels, step(): pl.pallas_call(step_kernel, out_shape=[jax.ShapeDtypeStruct((1, 1), F32),...  84.7 us
    pallas_call x1, Pallas kernels, build(): pl.pallas_call(build_kernel, out_shape=[piece] * 3, in_specs=[vmem] * 3,...  36.5 us
    unnamed x16, local copies, waits for them, and re-layouts  12.7 us

profile of v1, /device:TPU:1, one launch (start us, length us, event | category | flops | bytes accessed | tf_op | source)
XLA Modules:
  0.0 138.8 jit_solution(9752033171715155298)
XLA Ops:
  0.6 0.6 compare_reduce_fusion
  1.3 0.8 copy.12
  2.1 0.1 copy.15
  2.2 0.6 scatter.6.clone.w2t_ref
  2.8 0.7 broadcast_select_fusion
  3.5 0.6 scatter.9.w2_ref
  4.1 0.0 copy-start.3
  4.1 0.8 copy-done.3
  4.9 0.0 copy-start.4
  4.9 0.8 copy-done.4
  5.8 0.0 copy-start.5
  5.8 0.8 copy-done.5
  6.6 36.5 %build.1 = (bf16[2048,1024]{1,0:T(8,128)(2,1)S(1)}, bf16[2048,1024]{1,0:T(8,128)(2,1)S(1)}, bf16[2048,1024]{1,0:T(8,128)(2,1)S(1)}) custom-call(s32[128,128]{1,0:T(8,128)S(1)} %bitcast.9, s32[128,128]{1,0:T(8,128)S(1)} %bitcast.10, f32[128,128]{1,0:T(8,128)S(1)} %bitcast.11), custom_call_target="tpu_custom_call" | custom-call | tf_op jit(solution)/shard_map/build/pallas_call | solution.py:124
  43.1 0.0 copy-start
  43.1 1.9 %copy-done = bf16[2048,1024]{1,0:T(8,128)(2,1)} copy-done((bf16[2048,1024]{1,0:T(8,128)(2,1)}, bf16[2048,1024]{1,0:T(8,128)(2,1)S(1)}, u32[]{:S(2)}) %copy-start) | copy-done | bytes 4194328
  45.1 0.0 copy-start.1
  45.1 2.0 %copy-done.1 = bf16[2048,1024]{1,0:T(8,128)(2,1)} copy-done((bf16[2048,1024]{1,0:T(8,128)(2,1)}, bf16[2048,1024]{1,0:T(8,128)(2,1)S(1)}, u32[]{:S(2)}) %copy-start.1) | copy-done | bytes 4194328
  47.0 0.0 copy-start.2
  47.0 2.0 %copy-done.2 = bf16[2048,1024]{1,0:T(8,128)(2,1)} copy-done((bf16[2048,1024]{1,0:T(8,128)(2,1)}, bf16[2048,1024]{1,0:T(8,128)(2,1)S(1)}, u32[]{:S(2)}) %copy-start.2) | copy-done | bytes 4194328
  49.0 84.7 %step.1 = (f32[1,1]{1,0:T(1,128)}, f32[1024,128]{1,0:T(8,128)}, f32[128,19]{1,0:T(8,128)}) custom-call(bf16[1024,1024]{1,0:T(8,128)(2,1)} %x_ref.1, f32[1024,128]{1,0:T(8,128)} %w1_ref.1, bf16[32,128]{1,0:T(8,128)(2,1)} %scatter.6.clone.w2t_ref, bf16[128,32]{1,0:T(8,128)(2,1)} %scatter.9.w2_ref, s32[2,512]{1,0:T(2,128)} %send_ref.1, ...), custom_call_target="tpu_custom_call" | custom-call | tf_op jit(solution)/shard_map/step/pallas_call | solution.py:342
  133.7 1.5 %copy.14 = f32[128,19]{0,1:T(8,128)} copy(f32[128,19]{1,0:T(8,128)} %get-tuple-element.41) | data formatting | bytes 19456
  135.8 1.9 %copy.19 = f32[1024,128]{1,0:T(8,128)} copy(f32[1024,128]{1,0:T(8,128)} %get-tuple-element.46) | data formatting | bytes 1048576
Async XLA Ops:
  4.1 0.8 copy-start.3
  4.9 0.8 copy-start.4
  5.8 0.8 copy-start.5
  43.1 1.9 %copy-start = (bf16[2048,1024]{1,0:T(8,128)(2,1)}, bf16[2048,1024]{1,0:T(8,128)(2,1)S(1)}, u32[]{:S(2)}) copy-start(bf16[2048,1024]{1,0:T(8,128)(2,1)S(1)} %get-tuple-element.33.bh_ref) | copy-start | bytes 12582916
  45.1 2.0 %copy-start.1 = (bf16[2048,1024]{1,0:T(8,128)(2,1)}, bf16[2048,1024]{1,0:T(8,128)(2,1)S(1)}, u32[]{:S(2)}) copy-start(bf16[2048,1024]{1,0:T(8,128)(2,1)S(1)} %get-tuple-element.34.bm_ref) | copy-start | bytes 12582916
  47.0 2.0 %copy-start.2 = (bf16[2048,1024]{1,0:T(8,128)(2,1)}, bf16[2048,1024]{1,0:T(8,128)(2,1)S(1)}, u32[]{:S(2)}) copy-start(bf16[2048,1024]{1,0:T(8,128)(2,1)S(1)} %get-tuple-element.35.bl_ref) | copy-start | bytes 12582916

commit v2 on v1

--- a/solution.py
+++ b/solution.py
@@ -15,9 +15,8 @@
 EXT = NODES + 2 * HALO
 HID = 128
 PADC = 32
-BATCH = 128
-GROUP = 16
-NB = 4
+LAST = 8 * EXT
+NSM = 4
 ROW_N = (((1,), (0,)), ((), ()))
 ROW_T = (((1,), (1,)), ((), ()))
 
@@ -38,113 +37,122 @@
     return lax.dot_general(a, b, ROW_T, preferred_element_type=F32)
 
 
-def build_kernel(src_ref, dst_ref, w_ref, bh_ref, bm_ref, bl_ref, m_ref, rs0, rs1, row_v, wh, wm, wl, *rest):
-    us0, us1, sem = rest[:NB], rest[NB:2 * NB], rest[2 * NB]
-    n_batch = src_ref.shape[0]
-    row_v[...] = ((dst_ref[...] >> 7) << 11) + src_ref[...]
-    h, m, l = split3(w_ref[...])
-    wh[...] = h.astype(F32)
-    wm[...] = m.astype(F32)
-    wl[...] = l.astype(F32)
-    n_half = n_batch // NB
-
-    def rows_copy(i, rs, k):
-        return pltpu.make_async_copy(row_v.at[pl.ds(pl.multiple_of(i * NB, NB), NB), :], rs, sem.at[k])
-
-    rows_copy(0, rs0, 0).start()
-
+def build_kernel(src_hbm, dst_hbm, w_hbm, bh_ref, bm_ref, bl_ref, ma, mb, src_v, dst_v, w_v, row_v, lane_v, lane2_v, w2_v, left_v, ua, ub, *rest):
+    rss, sem, rsem = rest[:NSM], rest[NSM], rest[NSM + 1]
+    tiles = src_v.shape[0] // 8
+    loads = [pltpu.make_async_copy(a, b, sem.at[k]) for k, (a, b) in enumerate(((src_hbm, src_v), (dst_hbm, dst_v), (w_hbm, w_v)))]
+    for c in loads: c.start()
     def zero(i, c):
-        m_ref[pl.ds(pl.multiple_of(i * 256, 256), 256), :] = jnp.zeros((256, 128), F32)
-        return c
-
-    lax.fori_loop(0, m_ref.shape[0] // 256, zero, 0)
-    ii = lax.broadcasted_iota(jnp.int32, (BATCH, BATCH), 1)
-    jj = lax.broadcasted_iota(jnp.int32, (BATCH, BATCH), 0)
-    tri = jnp.logical_and(ii <= jj, (ii >> 4) == (jj >> 4))
-
-    def make_u(b, u):
-        rb = jnp.broadcast_to(row_v[pl.ds(b, 1), :], (BATCH, BATCH))
-        same = jnp.where(jnp.logical_and(rb == rb.T, tri), 1.0, 0.0).astype(BF16)
-        hit = jj == (dst_ref[pl.ds(b, 1), :] & 127)
-        acc = None
-        for piece in (wh, wm, wl):
-            v = jnp.where(hit, piece[pl.ds(b, 1), :], 0.0).astype(BF16)
-            d = dot_t(same, v)
-            acc = d if acc is None else acc + d
-        u[...] = acc
-
-    def rmw(k, rs, u):
-        for g in range(BATCH // GROUP):
-            rows = [rs[k, g * GROUP + j] for j in range(GROUP)]
-            vals = [m_ref[pl.ds(rows[j], 1), :] + u[pl.ds(g * GROUP + j, 1), :] for j in range(GROUP)]
-            for j in range(GROUP):
-                m_ref[pl.ds(rows[j], 1), :] = vals[j]
-
-    for k in range(NB):
-        make_u(k, us0[k])
-
-    def body(t, c):
-        b = 2 * NB * t
-        rows_copy(2 * t, rs0, 0).wait()
-        rows_copy(2 * t + 1, rs1, 1).start()
-        for k in range(NB):
-            make_u(b + NB + k, us1[k])
-        for k in range(NB):
-            rmw(k, rs0, us0[k])
-        rows_copy(2 * t + 1, rs1, 1).wait()
-        nxt = jnp.minimum(2 * t + 2, n_half - 1)
-        rows_copy(nxt, rs0, 0).start()
-        for k in range(NB):
-            make_u(nxt * NB + k, us0[k])
-        for k in range(NB):
-            rmw(k, rs1, us1[k])
-        return c
-
-    lax.fori_loop(0, n_half // 2, body, 0)
-    rows_copy(n_half - 1, rs0, 0).wait()
+        z = jnp.zeros((256, 128), F32)
+        rows = pl.ds(pl.multiple_of(i * 256, 256), 256)
+        ma[rows, :] = z; mb[rows, :] = z
+        return c
+    lax.fori_loop(0, LAST // 256, zero, 0)
+    for c in loads: c.wait()
+    sub = lax.broadcasted_iota(jnp.int32, (8, 128), 0)
+    def prep(t, left):
+        tile = pl.ds(pl.multiple_of(t * 8, 8), 8)
+        dst = dst_v[tile, :]
+        row = ((dst >> 7) << 11) + src_v[tile, :]
+        lane = (dst & 127).astype(F32)
+        w = w_v[tile, :]
+        seen = jnp.zeros((8, 128), F32); lane2 = seen; w2 = seen
+        for d in range(1, 8):
+            same = jnp.logical_and(row == pltpu.roll(row, d, axis=0), sub >= d)
+            seen = seen + jnp.where(same, 1.0, 0.0)
+            lane2 = lane2 + jnp.where(same, pltpu.roll(lane, d, axis=0), 0.0)
+            w2 = w2 + jnp.where(same, pltpu.roll(w, d, axis=0), 0.0)
+        late = seen > 1.5
+        row_v[tile, :] = jnp.where(late, LAST, row)
+        lane_v[tile, :] = lane
+        lane2_v[tile, :] = lane2
+        w2_v[tile, :] = w2
+        mark = jnp.where(late, 1.0, 0.0)
+        left_v[tile, :] = mark
+        return left + mark
+    left = lax.fori_loop(0, tiles, prep, jnp.zeros((8, 128), F32))
+    n_left = jnp.sum(left)
+
+    def rows_copy(t, rs, k):
+        return pltpu.make_async_copy(row_v.at[pl.ds(pl.multiple_of(t * 8, 8), 8), :], rs, rsem.at[k])
+    lanes = lax.broadcasted_iota(jnp.int32, (128, 128), 1).astype(F32)
+    def cols(t):
+        tile = pl.ds(pl.multiple_of(t * 8, 8), 8)
+        return [r[tile, :].T for r in (lane_v, w_v, lane2_v, w2_v)]
+    def make_u(cs, k, u):
+        l1, w1, l2, w2 = [jnp.broadcast_to(c[:, k:k + 1], (128, 128)) for c in cs]
+        u[k] = jnp.where(lanes == l1, w1, 0.0) + jnp.where(lanes == l2, w2, 0.0)
+    def rmw_half(rs, u, hooks):
+        pend = None
+        for j in range(129):
+            if j < 128:
+                m = ma if j % 2 == 0 else mb
+                rows = [rs[k, j] for k in range(8)]
+                vals = [m[pl.ds(rows[k], 1), :] + u[k, pl.ds(j, 1), :] for k in range(8)]
+            if pend is not None:
+                pm, prow, pval = pend
+                for k in range(8):
+                    pm[pl.ds(prow[k], 1), :] = pval[k]
+            if j < 128:
+                pend = (m, rows, vals)
+                if j % 16 == 0 and hooks: hooks[j // 16]()
+    def half(t, nxt, cur_u, nxt_u, cur_rs):
+        cs = cols(nxt)
+        hooks = [functools.partial(make_u, cs, k, nxt_u) for k in range(8)]
+        rmw_half(cur_rs, cur_u, hooks)
+    cs = cols(0)
+    for k in range(8): make_u(cs, k, ua)
+    NS = len(rss)
+    for q in range(NS - 1): rows_copy(q, rss[q], q).start()
+    def body(i, c):
+        for q in range(NS):
+            t = NS * i + q
+            rows_copy(t, rss[q], q).wait()
+            rows_copy(jnp.minimum(t + NS - 1, tiles - 1), rss[(q + NS - 1) % NS], (q + NS - 1) % NS).start()
+            half(t, jnp.minimum(t + 1, tiles - 1), (ua, ub)[q % 2], (ub, ua)[q % 2], rss[q])
+        return c
+    lax.fori_loop(0, tiles // NS, body, 0)
+    for q in range(NS - 1): rows_copy(tiles - 1, rss[q], q).wait()
+
+    pos = lax.broadcasted_iota(jnp.int32, (8 * tiles, 128), 0) * 128 + lax.broadcasted_iota(jnp.int32, (8 * tiles, 128), 1)
+    lane_row = lax.broadcasted_iota(jnp.int32, (1, 128), 1)
+    def one_left(i, c):
+        p = jnp.min(jnp.where(left_v[...] > 0.5, pos, 8 * tiles * 128).astype(F32)).astype(jnp.int32)
+        here = pos == p
+        left_v[...] = jnp.where(here, 0.0, left_v[...])
+        pick = lambda x: jnp.sum(jnp.where(here, x, 0.0))
+        dst = pick(dst_v[...].astype(F32)).astype(jnp.int32)
+        row = ((dst >> 7) << 11) + pick(src_v[...].astype(F32)).astype(jnp.int32)
+        ma[pl.ds(row, 1), :] = ma[pl.ds(row, 1), :] + jnp.where(lane_row == (dst & 127), pick(w_v[...]), 0.0)
+        return c
+    lax.fori_loop(0, n_left.astype(jnp.int32), one_left, 0)
 
     def out(i, c):
         rows = pl.ds(pl.multiple_of(i * 128, 128), 128)
         for j in range(NODES // 128):
-            h, m, l = split3(m_ref[pl.ds(pl.multiple_of(j * EXT + i * 128, 128), 128), :])
+            part = pl.ds(pl.multiple_of(j * EXT + i * 128, 128), 128)
+            h, m, l = split3(ma[part, :] + mb[part, :])
             cols = pl.ds(j * 128, 128)
-            bh_ref[rows, cols] = h
-            bm_ref[rows, cols] = m
-            bl_ref[rows, cols] = l
-        return c
-
+            bh_ref[rows, cols] = h; bm_ref[rows, cols] = m; bl_ref[rows, cols] = l
+        return c
     lax.fori_loop(0, EXT // 128, out, 0)
-
-
-def build(src, dst, w):
-    n = src.shape[0]
-    nb = n // BATCH
-    piece = jax.ShapeDtypeStruct((EXT, NODES), BF16)
-    vmem = pl.BlockSpec(memory_space=pltpu.VMEM)
-    return pl.pallas_call(
-        build_kernel,
-        out_shape=[piece] * 3,
-        in_specs=[vmem] * 3,
-        out_specs=[vmem] * 3,
-        scratch_shapes=[
-            pltpu.VMEM((8 * EXT, 128), F32),
-            pltpu.SMEM((NB, BATCH), jnp.int32),
-            pltpu.SMEM((NB, BATCH), jnp.int32),
-            pltpu.VMEM((nb, BATCH), jnp.int32),
-        ]
-        + [pltpu.VMEM((nb, BATCH), F32)] * 3
-        + [pltpu.VMEM((BATCH, 128), F32)] * (2 * NB)
-        + [pltpu.SemaphoreType.DMA((2,))],
-        name="build",
-        compiler_params=pltpu.CompilerParams(vmem_limit_bytes=40 * 1024 * 1024),
-    )(src.reshape(nb, BATCH), dst.reshape(nb, BATCH), w.reshape(nb, BATCH))
+def build(src,dst,w):
+    n=src.shape[0]; nb=n//128
+    s2=lambda a:pltpu.with_memory_space_constraint(a.reshape(nb,128), pltpu.HBM)
+    o=jax.ShapeDtypeStruct((EXT,NODES),BF16)
+    V=pl.BlockSpec(memory_space=pltpu.VMEM); H=pl.BlockSpec(memory_space=pltpu.HBM)
+    S=pltpu.VMEM
+    return pl.pallas_call(build_kernel, out_shape=[o]*3, in_specs=[H]*3, out_specs=[V]*3,
+        scratch_shapes=[S((LAST+8,128),F32)]*2+[S((nb,128),jnp.int32)]*2+[S((nb,128),F32)]+[S((nb,128),jnp.int32)]+[S((nb,128),F32)]*4
+          +[S((8,128,128),F32)]*2+[pltpu.SMEM((8,128),jnp.int32)]*NSM+[pltpu.SemaphoreType.DMA((3,)),pltpu.SemaphoreType.DMA((NSM,))],
+        name="build", cost_estimate=pl.CostEstimate(flops=10**10, bytes_accessed=80 * 10**6, transcendentals=0), compiler_params=pltpu.CompilerParams(vmem_limit_bytes=36*1024*1024))(s2(src),s2(dst),s2(w))
 
 
 def step_kernel(
-    x_ref, w1_ref, w2t_ref, w2_ref, send_ref, bh_ref, bm_ref, bl_ref, lab_ref, mask_ref,
+    x_ref, w1_ref, w2_ref, send_ref, bh_ref, bm_ref, bl_ref, lab_ref, mask_ref,
     loss_ref, out_ref, two_ref,
     s0_ref, s1_ref, sb1, hp1, hn1, sb2, hp2, hn2, gb2, ra2, rb2, gb1, ra1, rb1,
-    y_ref, hid_ref, part, rc, a1, rx, a2, ry, a3, rz, cnt, cntr, sml, smlr, own_ref, dy_ref, ssem, rsem,
+    y_ref, hid_ref, part, rc, a1, rx, a2, ry, a3, rz, cnt, cntr, sml, smlr, own_ref, dy_ref, w2p, ssem, rsem,
 ):
     me = lax.axis_index(AXIS)
     num = 128
@@ -199,6 +207,10 @@
 
     cc = small_start(cnt, cntr, 0)
 
+    w2p[...] = jnp.zeros((HID, HID), F32)
+    w2p[:, 0:19] = w2_ref[...]
+    w2t = w2p[...].T.astype(BF16)[0:PADC, :]
+
     node = lax.broadcasted_iota(jnp.int32, (NODES, HALO), 0)
     s0_ref[...] = jnp.where(node == send_ref[0:1, :], 1.0, 0.0).astype(BF16)
     s1_ref[...] = jnp.where(node == send_ref[1:2, :], 1.0, 0.0).astype(BF16)
@@ -226,7 +238,7 @@
     cc = small_start(cnt, cntr, 2)
     hid = jnp.maximum(y, 0.0).astype(BF16)
     hid_ref[...] = hid
-    t2 = dot_n(w2t_ref[...], hid).astype(BF16)
+    t2 = dot_n(w2t, hid).astype(BF16)
     sb2[1] = dot_n(t2, s1_ref[...]).astype(BF16)
     sb2[0] = dot_n(t2, s0_ref[...]).astype(BF16)
     c_p = copy(sb2.at[1], hp2, nxt)
@@ -276,7 +288,7 @@
     sml[...] = g2
     sml[24:32, :] = jnp.broadcast_to(loss, (8, 128))
     cs = small_start(sml, smlr, 0)
-    dh = dot_n(w2_ref[...], dt2)
+    dh = dot_n(w2p[:, 0:PADC].astype(BF16), dt2)
     dy_ref[...] = jnp.where(y_ref[...] > 0.0, dh, 0.0)
     gb1[0] = agg_back(dy_ref[...], NODES, NODES + HALO)
     c_p = copy(gb1.at[0], ra1, prv)
@@ -327,15 +339,12 @@
     half = out_ref.at[mine]
     last = copy(half, half, twin)
     loss_ref[...] = sml[24:25, 0:1] / count
-    two_ref[...] = sml[...].T[:, 0:19]
+    two_ref[...] = sml[0:19, :]
     last.wait()
 
 
 def step(x, w_one, w_two, send_rows, src, dst, w, labels, mask):
     bh, bm, bl = build(src, dst, w)
-    w2 = w_two.astype(BF16)
-    w2t = jnp.zeros((PADC, HID), BF16).at[:19, :].set(w2.T)
-    w2p = jnp.zeros((HID, PADC), BF16).at[:, :19].set(w2)
     vmem = pl.BlockSpec(memory_space=pltpu.VMEM)
     n_sem = 10 + 4 + 4 + 10 + 20
     V = pltpu.VMEM
@@ -344,9 +353,9 @@
         out_shape=[
             jax.ShapeDtypeStruct((1, 1), F32),
             jax.ShapeDtypeStruct((1024, HID), F32),
-            jax.ShapeDtypeStruct((HID, 19), F32),
+            jax.ShapeDtypeStruct((19, HID), F32),
         ],
-        in_specs=[vmem] * 10,
+        in_specs=[vmem] * 9,
         out_specs=[vmem] * 3,
         scratch_shapes=[
             V((NODES, HALO), BF16), V((NODES, HALO), BF16),
@@ -358,15 +367,15 @@
             V((1024, HID), F32), V((512, HID), F32), V((512, HID), F32),
             V((3, 128, HID), F32), V((128, HID), F32), V((3, 32, HID), F32), V((32, HID), F32), V((3, 8, HID), F32),
             V((8, 128), F32), V((4, 4, 8, 128), F32), V((PADC, 128), F32), V((4, 4, PADC, 128), F32),
-            V((HID, NODES), F32), V((HID, NODES), F32),
+            V((HID, NODES), F32), V((HID, NODES), F32), V((HID, HID), F32),
             pltpu.SemaphoreType.DMA((n_sem,)), pltpu.SemaphoreType.DMA((n_sem,)),
         ],
         name="step",
         compiler_params=pltpu.CompilerParams(
-            collective_id=0, has_side_effects=True, vmem_limit_bytes=56 * 1024 * 1024
+            collective_id=0, has_side_effects=True, vmem_limit_bytes=28 * 1024 * 1024
         ),
-    )(x, w_one, w2t, w2p, send_rows, bh, bm, bl, labels.reshape(1, NODES), mask.reshape(1, NODES))
-    return loss.reshape(()), one, two
+    )(x, w_one, w_two, send_rows, bh, bm, bl, labels.reshape(1, NODES), mask.reshape(1, NODES))
+    return loss.reshape(()), one, two.T
 
 
 def solution(mesh):

time: 139 us -> 105 us (0.76)
  Pallas kernels: 121 us -> 100 us
  local copies, waits for them, and re-layouts: 13.9 us -> 2.23 us
    pallas_call x1, Pallas kernels: 36.5 us -> 21.1 us  [build(): pl.pallas_call(build_kernel, out_shape=[o] * 3, in_specs=[H] * 3, out_spe...]
    unnamed x16 -> x13, local copies, waits for them, and re-layouts: 12.7 us -> 2.23 us
    pallas_call x1, Pallas kernels: 84.7 us -> 79.1 us  [step(): pl.pallas_call(step_kernel, out_shape=[jax.ShapeDtypeStruct((1, 1), F32),...]
where the time goes in v2:
time: 105 us
  Pallas kernels  100 us (95%)
  between operations  2.54 us (2%)
  local copies, waits for them, and re-layouts  2.23 us (2%)
    pallas_call x1, Pallas kernels, step(): pl.pallas_call(step_kernel, out_shape=[jax.ShapeDtypeStruct((1, 1), F32),...  79.1 us
    pallas_call x1, Pallas kernels, build(): pl.pallas_call(build_kernel, out_shape=[o] * 3, in_specs=[H] * 3, out_spe...  21.1 us
    unnamed x13, local copies, waits for them, and re-layouts  2.23 us

profile of v2, /device:TPU:1, one launch (start us, length us, event | category | flops | bytes accessed | tf_op | source)
XLA Modules:
  0.0 105.0 jit_solution(11059167215363304392)
XLA Ops:
  0.6 0.8 copy.12.w2_ref
  1.4 0.0 copy-start
  1.4 0.0 copy-start.1
  1.5 0.0 copy-start.2
  1.5 0.0 copy-start.3
  1.5 0.0 copy-start.4
  1.5 21.1 %build.1 = (bf16[2048,1024]{1,0:T(8,128)(2,1)S(1)}, bf16[2048,1024]{1,0:T(8,128)(2,1)S(1)}, bf16[2048,1024]{1,0:T(8,128)(2,1)S(1)}) custom-call(s32[128,128]{1,0:T(8,128)} %bitcast.10, s32[128,128]{1,0:T(8,128)} %bitcast.11, f32[128,128]{1,0:T(8,128)} %bitcast.12), custom_call_target="tpu_custom_call" | custom-call | flops 10000000000 | bytes 80000000 | tf_op jit(solution)/shard_map/build/pallas_call | solution.py:145
  22.6 0.0 copy-done
  22.6 0.0 copy-done.1
  22.6 0.0 copy-done.2
  22.6 0.0 copy-done.3
  22.6 0.0 copy-done.4
  22.6 79.1 %step.1 = (f32[1,1]{1,0:T(1,128)}, f32[1024,128]{1,0:T(8,128)S(1)}, f32[19,128]{1,0:T(8,128)S(1)}) custom-call(bf16[1024,1024]{1,0:T(8,128)(2,1)S(1)} %copy-done, f32[1024,128]{1,0:T(8,128)S(1)} %copy-done.1, f32[128,19]{1,0:T(8,128)S(1)} %copy.12.w2_ref, s32[2,512]{1,0:T(2,128)S(1)} %copy-done.2, bf16[2048,1024]{1,0:T(8,128)(2,1)S(1)} %get-tuple-element.9.bh_ref, ...), custom_call_target="tpu_custom_call" | custom-call | tf_op jit(solution)/shard_map/step/pallas_call | solution.py:351
  102.4 0.8 copy.17
  103.2 0.6 copy.18
Async XLA Ops:
  1.4 21.2 %copy-start = (bf16[1024,1024]{1,0:T(8,128)(2,1)S(1)}, bf16[1024,1024]{1,0:T(8,128)(2,1)}, u32[]{:S(2)}) copy-start(bf16[1024,1024]{1,0:T(8,128)(2,1)} %x_ref.1) | copy-start | bytes 6291460
  1.4 21.2 %copy-start.1 = (f32[1024,128]{1,0:T(8,128)S(1)}, f32[1024,128]{1,0:T(8,128)}, u32[]{:S(2)}) copy-start(f32[1024,128]{1,0:T(8,128)} %w1_ref.1) | copy-start | bytes 1572868
  1.5 21.2 %copy-start.2 = (s32[2,512]{1,0:T(2,128)S(1)}, s32[2,512]{1,0:T(2,128)}, u32[]{:S(2)}) copy-start(s32[2,512]{1,0:T(2,128)} %send_ref.1) | copy-start | bytes 12292
  1.5 21.2 %copy-start.3 = (s32[1024]{0:T(1024)S(1)}, s32[1024]{0:T(1024)}, u32[]{:S(2)}) copy-start(s32[1024]{0:T(1024)} %param.16) | copy-start | bytes 12292
  1.5 21.2 %copy-start.4 = (s32[1024]{0:T(1024)S(1)}, s32[1024]{0:T(1024)}, u32[]{:S(2)}) copy-start(s32[1024]{0:T(1024)} %param.17) | copy-start | bytes 12292

commit v3 on v2

--- a/solution.py
+++ b/solution.py
@@ -17,6 +17,7 @@
 PADC = 32
 LAST = 8 * EXT
 NSM = 4
+CHIPS = 64
 ROW_N = (((1,), (0,)), ((), ()))
 ROW_T = (((1,), (1,)), ((), ()))
 
@@ -37,7 +38,7 @@
     return lax.dot_general(a, b, ROW_T, preferred_element_type=F32)
 
 
-def build_kernel(src_hbm, dst_hbm, w_hbm, bh_ref, bm_ref, bl_ref, ma, mb, src_v, dst_v, w_v, row_v, lane_v, lane2_v, w2_v, left_v, ua, ub, *rest):
+def build_kernel(src_hbm, dst_hbm, w_hbm, ma, mb, src_v, dst_v, w_v, row_v, lane_v, lane2_v, w2_v, left_v, ua, ub, *rest):
     rss, sem, rsem = rest[:NSM], rest[NSM], rest[NSM + 1]
     tiles = src_v.shape[0] // 8
     loads = [pltpu.make_async_copy(a, b, sem.at[k]) for k, (a, b) in enumerate(((src_hbm, src_v), (dst_hbm, dst_v), (w_hbm, w_v)))]
@@ -127,32 +128,24 @@
         return c
     lax.fori_loop(0, n_left.astype(jnp.int32), one_left, 0)
 
-    def out(i, c):
-        rows = pl.ds(pl.multiple_of(i * 128, 128), 128)
-        for j in range(NODES // 128):
-            part = pl.ds(pl.multiple_of(j * EXT + i * 128, 128), 128)
-            h, m, l = split3(ma[part, :] + mb[part, :])
-            cols = pl.ds(j * 128, 128)
-            bh_ref[rows, cols] = h; bm_ref[rows, cols] = m; bl_ref[rows, cols] = l
-        return c
-    lax.fori_loop(0, EXT // 128, out, 0)
+
 def build(src,dst,w):
     n=src.shape[0]; nb=n//128
     s2=lambda a:pltpu.with_memory_space_constraint(a.reshape(nb,128), pltpu.HBM)
-    o=jax.ShapeDtypeStruct((EXT,NODES),BF16)
+    o=jax.ShapeDtypeStruct((LAST+8,128),F32)
     V=pl.BlockSpec(memory_space=pltpu.VMEM); H=pl.BlockSpec(memory_space=pltpu.HBM)
     S=pltpu.VMEM
-    return pl.pallas_call(build_kernel, out_shape=[o]*3, in_specs=[H]*3, out_specs=[V]*3,
-        scratch_shapes=[S((LAST+8,128),F32)]*2+[S((nb,128),jnp.int32)]*2+[S((nb,128),F32)]+[S((nb,128),jnp.int32)]+[S((nb,128),F32)]*4
+    return pl.pallas_call(build_kernel, out_shape=[o]*2, in_specs=[H]*3, out_specs=[V]*2,
+        scratch_shapes=[S((nb,128),jnp.int32)]*2+[S((nb,128),F32)]+[S((nb,128),jnp.int32)]+[S((nb,128),F32)]*4
           +[S((8,128,128),F32)]*2+[pltpu.SMEM((8,128),jnp.int32)]*NSM+[pltpu.SemaphoreType.DMA((3,)),pltpu.SemaphoreType.DMA((NSM,))],
         name="build", cost_estimate=pl.CostEstimate(flops=10**10, bytes_accessed=80 * 10**6, transcendentals=0), compiler_params=pltpu.CompilerParams(vmem_limit_bytes=36*1024*1024))(s2(src),s2(dst),s2(w))
 
 
 def step_kernel(
-    x_ref, w1_ref, w2_ref, send_ref, bh_ref, bm_ref, bl_ref, lab_ref, mask_ref,
+    x_ref, w1_ref, w2_ref, send_ref, ma_ref, mb_ref, lab_ref, mask_ref,
     loss_ref, out_ref, two_ref,
     s0_ref, s1_ref, sb1, hp1, hn1, sb2, hp2, hn2, gb2, ra2, rb2, gb1, ra1, rb1,
-    y_ref, hid_ref, part, rc, a1, rx, a2, ry, a3, rz, cnt, cntr, sml, smlr, own_ref, dy_ref, w2p, ssem, rsem,
+    y_ref, hid_ref, part, rc, a1, rx, cnt, cntr, sml, smlr, own_ref, dy_ref, w2p, bh_ref, bm_ref, bl_ref, ssem, rsem, fsem, frsem, gsem, grsem,
 ):
     me = lax.axis_index(AXIS)
     num = 128
@@ -174,7 +167,6 @@
     targets = [nxt, prv, twin] + [peer(k, d)[1] for k in range(3) for d in (1, 2, 3)]
     for t in targets:
         pl.semaphore_signal(barrier, inc=1, device_id=(t,), device_id_type=pl.DeviceIdType.MESH)
-    pl.semaphore_wait(barrier, len(targets))
 
     counter = [0]
 
@@ -205,11 +197,11 @@
         else:
             val[...] = (recv[stage, 0] + recv[stage, 1]) + (recv[stage, 2] + recv[stage, 3])
 
-    cc = small_start(cnt, cntr, 0)
 
     w2p[...] = jnp.zeros((HID, HID), F32)
-    w2p[:, 0:19] = w2_ref[...]
-    w2t = w2p[...].T.astype(BF16)[0:PADC, :]
+    w2p[0:19, :] = w2_ref[...]
+    w2t = w2p[0:PADC, :].astype(BF16)
+    w2n = w2p[...].T.astype(BF16)[:, 0:PADC]
 
     node = lax.broadcasted_iota(jnp.int32, (NODES, HALO), 0)
     s0_ref[...] = jnp.where(node == send_ref[0:1, :], 1.0, 0.0).astype(BF16)
@@ -219,15 +211,30 @@
     t1 = t1.T.astype(BF16)
     sb1[1] = dot_n(t1, s1_ref[...]).astype(BF16)
     sb1[0] = dot_n(t1, s0_ref[...]).astype(BF16)
+    pl.semaphore_wait(barrier, len(targets))
     c_p = copy(sb1.at[1], hp1, nxt)
     c_n = copy(sb1.at[0], hn1, prv)
+    cc = small_start(cnt, cntr, 0)
 
     def agg(e, lo, hi):
         acc = dot_n(e, bl_ref[lo:hi, :])
         acc = acc + dot_n(e, bm_ref[lo:hi, :])
         return acc + dot_n(e, bh_ref[lo:hi, :])
 
+    def split_rows(i, c):
+        rows = pl.ds(pl.multiple_of(i * 128, 128), 128)
+        for j in range(NODES // 128):
+            part_rows = pl.ds(pl.multiple_of(j * EXT + i * 128, 128), 128)
+            h, m, l = split3(ma_ref[part_rows, :] + mb_ref[part_rows, :])
+            cols = pl.ds(j * 128, 128)
+            bh_ref[rows, cols] = h
+            bm_ref[rows, cols] = m
+            bl_ref[rows, cols] = l
+        return c
+
+    lax.fori_loop(0, NODES // 128, split_rows, 0)
     y_ref[...] = agg(t1, 0, NODES)
+    lax.fori_loop(NODES // 128, EXT // 128, split_rows, 0)
     small_end(cc, cnt, cntr, 0)
     cc = small_start(cnt, cntr, 1)
     c_p.wait()
@@ -288,7 +295,7 @@
     sml[...] = g2
     sml[24:32, :] = jnp.broadcast_to(loss, (8, 128))
     cs = small_start(sml, smlr, 0)
-    dh = dot_n(w2p[:, 0:PADC].astype(BF16), dt2)
+    dh = dot_n(w2n, dt2)
     dy_ref[...] = jnp.where(y_ref[...] > 0.0, dh, 0.0)
     gb1[0] = agg_back(dy_ref[...], NODES, NODES + HALO)
     c_p = copy(gb1.at[0], ra1, prv)
@@ -311,31 +318,52 @@
     copy(part.at[other], rc, twin).wait()
     a1[...] = part[mine, :] + rc[...]
 
-    def scatter_stage(dim, val, recv, size, res):
-        c, _ = dims[dim]
-        cps = []
-        for d in (1, 2, 3):
-            p, dev = peer(dim, d)
-            cps.append(copy(val.at[pl.ds(pl.multiple_of(p * size, size), size)], recv.at[d - 1], dev))
-        for k in cps:
-            k.wait()
-        res[...] = (val[pl.ds(pl.multiple_of(c * size, size), size), :] + recv[0]) + (recv[1] + recv[2])
-
-    scatter_stage(0, a1, rx, 128, a2)
+    chip = me // 2
+
+    def rows_of(q):
+        return pl.ds(pl.multiple_of(q * 8, 8), 8)
+
+    def far(i):
+        d = lax.rem(i + 41, CHIPS - 1) + 1
+        q = lax.rem(chip + d, CHIPS)
+        return d - 1, q, q * 2 + core
+
+    def scatter_copy(i):
+        k, q, dev = far(i)
+        return pltpu.make_async_remote_copy(
+            src_ref=a1.at[rows_of(q)], dst_ref=rx.at[k], send_sem=fsem.at[k], recv_sem=frsem.at[k],
+            device_id=(dev,), device_id_type=pl.DeviceIdType.MESH,
+        )
+
+    def gather_copy(i):
+        k, q, dev = far(i)
+        rows = out_ref.at[pl.ds(pl.multiple_of(core * 512 + chip * 8, 8), 8)]
+        return pltpu.make_async_remote_copy(
+            src_ref=rows, dst_ref=rows, send_sem=gsem.at[k], recv_sem=grsem.at[k],
+            device_id=(dev,), device_id_type=pl.DeviceIdType.MESH,
+        )
+
+    def start_all(make):
+        def one(i, c):
+            make(i).start()
+            return c
+        lax.fori_loop(0, CHIPS - 1, one, 0)
+
+    def wait_all(make):
+        def one(i, c):
+            make(i).wait()
+            return c
+        lax.fori_loop(0, CHIPS - 1, one, 0)
+
+    start_all(scatter_copy)
     small_end(cs, sml, smlr, 3)
-    scatter_stage(1, a2, ry, 32, a3)
-    spot = core * 512 + cx * 128 + cy * 32 + cz * 8
-    scatter_stage(2, a3, rz, 8, out_ref.at[pl.ds(pl.multiple_of(spot, 8), 8)])
-
-    def gather_stage(dim, start, size):
-        rows = out_ref.at[pl.ds(pl.multiple_of(start, size), size)]
-        cps = [copy(rows, rows, peer(dim, d)[1]) for d in (1, 2, 3)]
-        for k in cps:
-            k.wait()
-
-    gather_stage(2, spot, 8)
-    gather_stage(1, core * 512 + cx * 128 + cy * 32, 32)
-    gather_stage(0, core * 512 + cx * 128, 128)
+    wait_all(scatter_copy)
+    total = a1[rows_of(chip), :]
+    for k in range(CHIPS - 1):
+        total = total + rx[k]
+    out_ref[pl.ds(pl.multiple_of(core * 512 + chip * 8, 8), 8), :] = total
+    start_all(gather_copy)
+    wait_all(gather_copy)
     half = out_ref.at[mine]
     last = copy(half, half, twin)
     loss_ref[...] = sml[24:25, 0:1] / count
@@ -344,9 +372,9 @@
 
 
 def step(x, w_one, w_two, send_rows, src, dst, w, labels, mask):
-    bh, bm, bl = build(src, dst, w)
+    ma, mb = build(src, dst, w)
     vmem = pl.BlockSpec(memory_space=pltpu.VMEM)
-    n_sem = 10 + 4 + 4 + 10 + 20
+    n_sem = 30
     V = pltpu.VMEM
     loss, one, two = pl.pallas_call(
         step_kernel,
@@ -355,7 +383,7 @@
             jax.ShapeDtypeStruct((1024, HID), F32),
             jax.ShapeDtypeStruct((19, HID), F32),
         ],
-        in_specs=[vmem] * 9,
+        in_specs=[vmem] * 8,
         out_specs=[vmem] * 3,
         scratch_shapes=[
             V((NODES, HALO), BF16), V((NODES, HALO), BF16),
@@ -365,16 +393,18 @@
             V((2, HID, HALO), F32), V((HID, HALO), F32), V((HID, HALO), F32),
             V((HID, NODES), F32), V((HID, NODES), BF16),
             V((1024, HID), F32), V((512, HID), F32), V((512, HID), F32),
-            V((3, 128, HID), F32), V((128, HID), F32), V((3, 32, HID), F32), V((32, HID), F32), V((3, 8, HID), F32),
+            V((CHIPS - 1, 8, HID), F32),
             V((8, 128), F32), V((4, 4, 8, 128), F32), V((PADC, 128), F32), V((4, 4, PADC, 128), F32),
             V((HID, NODES), F32), V((HID, NODES), F32), V((HID, HID), F32),
+            V((EXT, NODES), BF16), V((EXT, NODES), BF16), V((EXT, NODES), BF16),
             pltpu.SemaphoreType.DMA((n_sem,)), pltpu.SemaphoreType.DMA((n_sem,)),
+            *[pltpu.SemaphoreType.DMA((CHIPS - 1,))] * 4,
         ],
         name="step",
         compiler_params=pltpu.CompilerParams(
-            collective_id=0, has_side_effects=True, vmem_limit_bytes=28 * 1024 * 1024
+            collective_id=0, has_side_effects=True, vmem_limit_bytes=31 * 1024 * 1024
         ),
-    )(x, w_one, w_two, send_rows, bh, bm, bl, labels.reshape(1, NODES), mask.reshape(1, NODES))
+    )(x, w_one, w_two.T, send_rows, ma, mb, labels.reshape(1, NODES), mask.reshape(1, NODES))
     return loss.reshape(()), one, two.T
 
 

time: 105 us -> 89.7 us (0.85)
  Pallas kernels: 100 us -> 85.7 us
    pallas_call x1, Pallas kernels: 79.1 us -> 67.8 us  [step(): pl.pallas_call(step_kernel, out_shape=[jax.ShapeDtypeStruct((1, 1), F32),...]
    pallas_call x1, Pallas kernels: 21.1 us -> 17.9 us  [build(): pl.pallas_call(build_kernel, out_shape=[o] * 2, in_specs=[H] * 3, out_spe...]
    unnamed x13 -> x14, local copies, waits for them, and re-layouts: 2.23 us -> 1.42 us
where the time goes in v3:
time: 89.7 us; the launch traced here: 89.6 us
  Pallas kernels  85.7 us (96%)
  between operations  2.43 us (3%)
  local copies, waits for them, and re-layouts  1.42 us (2%)
    pallas_call x1, Pallas kernels, step(): pl.pallas_call(step_kernel, out_shape=[jax.ShapeDtypeStruct((1, 1), F32),...  67.8 us
    pallas_call x1, Pallas kernels, build(): pl.pallas_call(build_kernel, out_shape=[o] * 2, in_specs=[H] * 3, out_spe...  17.9 us

profile of v3, /device:TPU:1, one launch (start us, length us, event | category | flops | bytes accessed | tf_op | source)
XLA Modules:
  0.0 89.6 jit_solution(9105572543014912548)
XLA Ops:
  0.6 0.0 copy-start
  0.6 0.0 copy-start.1
  0.7 0.0 copy-start.2
  0.7 0.0 copy-start.3
  0.7 0.0 copy-start.4
  0.7 0.0 copy-start.5
  0.7 17.9 %build.1 = (f32[16392,128]{1,0:T(8,128)S(1)}, f32[16392,128]{1,0:T(8,128)S(1)}) custom-call(s32[128,128]{1,0:T(8,128)} %bitcast.12, s32[128,128]{1,0:T(8,128)} %bitcast.13, f32[128,128]{1,0:T(8,128)} %bitcast.14), custom_call_target="tpu_custom_call" | custom-call | flops 10000000000 | bytes 80000000 | tf_op jit(solution)/shard_map/build/pallas_call | solution.py:138
  18.6 0.0 copy-done
  18.6 0.0 copy-done.1
  18.6 0.0 copy-done.2
  18.7 0.0 copy-done.3
  18.7 0.0 copy-done.4
  18.7 0.0 copy-done.5
  18.7 67.8 %step.1 = (f32[1,1]{1,0:T(1,128)}, f32[1024,128]{1,0:T(8,128)S(1)}, f32[19,128]{1,0:T(8,128)S(1)}) custom-call(bf16[1024,1024]{1,0:T(8,128)(2,1)S(1)} %copy-done, f32[1024,128]{1,0:T(8,128)S(1)} %copy-done.1, f32[19,128]{1,0:T(8,128)S(1)} %bitcast.8, s32[2,512]{1,0:T(2,128)S(1)} %copy-done.3, f32[16392,128]{1,0:T(8,128)S(1)} %get-tuple-element.8.ma_ref, ...), custom_call_target="tpu_custom_call" | custom-call | tf_op jit(solution)/shard_map/step/pallas_call | solution.py:379
  87.1 0.8 copy.16
  87.9 0.6 copy.17
Async XLA Ops:
  0.6 18.0 %copy-start = (bf16[1024,1024]{1,0:T(8,128)(2,1)S(1)}, bf16[1024,1024]{1,0:T(8,128)(2,1)}, u32[]{:S(2)}) copy-start(bf16[1024,1024]{1,0:T(8,128)(2,1)} %x_ref.1) | copy-start | bytes 6291460
  0.6 18.0 %copy-start.1 = (f32[1024,128]{1,0:T(8,128)S(1)}, f32[1024,128]{1,0:T(8,128)}, u32[]{:S(2)}) copy-start(f32[1024,128]{1,0:T(8,128)} %w1_ref.1) | copy-start | bytes 1572868
  0.7 18.0 %copy-start.2 = (f32[128,19]{0,1:T(8,128)S(1)}, f32[128,19]{0,1:T(8,128)}, u32[]{:S(2)}) copy-start(f32[128,19]{0,1:T(8,128)} %param.11) | copy-start | bytes 29188
  0.7 18.0 %copy-start.3 = (s32[2,512]{1,0:T(2,128)S(1)}, s32[2,512]{1,0:T(2,128)}, u32[]{:S(2)}) copy-start(s32[2,512]{1,0:T(2,128)} %send_ref.1) | copy-start | bytes 12292
  0.7 18.0 %copy-start.4 = (s32[1024]{0:T(1024)S(1)}, s32[1024]{0:T(1024)}, u32[]{:S(2)}) copy-start(s32[1024]{0:T(1024)} %param.16) | copy-start | bytes 12292
  0.7 18.0 %copy-start.5 = (s32[1024]{0:T(1024)S(1)}, s32[1024]{0:T(1024)}, u32[]{:S(2)}) copy-start(s32[1024]{0:T(1024)} %param.17) | copy-start | bytes 12292

commit v4 on v3

--- a/solution.py
+++ b/solution.py
@@ -12,6 +12,7 @@
 BF16 = jnp.bfloat16
 NODES = 1024
 HALO = 512
+QTR = HALO // 2
 EXT = NODES + 2 * HALO
 HID = 128
 PADC = 32
@@ -297,84 +298,86 @@
     cs = small_start(sml, smlr, 0)
     dh = dot_n(w2n, dt2)
     dy_ref[...] = jnp.where(y_ref[...] > 0.0, dh, 0.0)
-    gb1[0] = agg_back(dy_ref[...], NODES, NODES + HALO)
-    c_p = copy(gb1.at[0], ra1, prv)
-    gb1[1] = agg_back(dy_ref[...], NODES + HALO, EXT)
-    c_n = copy(gb1.at[1], rb1, nxt)
+    back = []
+    for h in range(2):
+        gb1[0, h] = agg_back(dy_ref[...], NODES + h * QTR, NODES + (h + 1) * QTR)
+        back.append(copy(gb1.at[0, h], ra1.at[h], prv))
+        gb1[1, h] = agg_back(dy_ref[...], NODES + HALO + h * QTR, NODES + HALO + (h + 1) * QTR)
+        back.append(copy(gb1.at[1, h], rb1.at[h], nxt))
     small_end(cs, sml, smlr, 0)
     cs = small_start(sml, smlr, 1)
     own_ref[...] = agg_back(dy_ref[...], 0, NODES)
     small_end(cs, sml, smlr, 1)
     cs = small_start(sml, smlr, 2)
-    c_p.wait()
-    c_n.wait()
-    dt1 = (own_ref[...] + (returned(ra1[...], s1_ref) + returned(rb1[...], s0_ref))).astype(BF16)
+    for h in range(2):
+        cols = pl.ds(h * QTR, QTR)
+        back[2 * h].wait()
+        back[2 * h + 1].wait()
+        own_ref[...] += returned(ra1[h], s1_ref.at[:, cols]) + returned(rb1[h], s0_ref.at[:, cols])
+    dt1 = own_ref[...].astype(BF16)
+
+    mine = pl.ds(pl.multiple_of(core * 512, 512), 512)
+    other = pl.ds(pl.multiple_of((1 - core) * 512, 512), 512)
+    part[...] = dot_n(dt1, x_ref[:, other]).T
+    swap = copy(part, rc, twin)
     small_end(cs, sml, smlr, 2)
     cs = small_start(sml, smlr, 3)
-    part[...] = dot_n(dt1, x_ref[...]).T
-
-    mine = pl.ds(pl.multiple_of(core * 512, 512), 512)
-    other = pl.ds(pl.multiple_of((1 - core) * 512, 512), 512)
-    copy(part.at[other], rc, twin).wait()
-    a1[...] = part[mine, :] + rc[...]
+    own_half = dot_n(dt1, x_ref[:, mine]).T
+    swap.wait()
+    a1[...] = own_half + rc[...]
 
     chip = me // 2
 
     def rows_of(q):
         return pl.ds(pl.multiple_of(q * 8, 8), 8)
 
-    def far(i):
-        d = lax.rem(i + 41, CHIPS - 1) + 1
-        q = lax.rem(chip + d, CHIPS)
-        return d - 1, q, q * 2 + core
-
-    def scatter_copy(i):
-        k, q, dev = far(i)
+    spot = lax.rem(chip, 16)
+    mine8 = pl.ds(pl.multiple_of(core * 512 + chip * 8, 8), 8)
+    shifts = [(dz, dr) for dz in (2, 1, 3, 0) for dr in range(16) if dz + dr > 0]
+
+    def far(dz, dr):
+        q = lax.rem(cz + dz, 4) * 16 + lax.rem(spot + dr, 16)
+        return dz * 16 + dr - 1, q, q * 2 + core
+
+    def far_copy(dz, dr, gather):
+        k, q, dev = far(dz, dr)
+        src = out_ref.at[mine8] if gather else a1.at[rows_of(q)]
         return pltpu.make_async_remote_copy(
-            src_ref=a1.at[rows_of(q)], dst_ref=rx.at[k], send_sem=fsem.at[k], recv_sem=frsem.at[k],
+            src_ref=src, dst_ref=src if gather else rx.at[k],
+            send_sem=(gsem if gather else fsem).at[k], recv_sem=(grsem if gather else frsem).at[k],
             device_id=(dev,), device_id_type=pl.DeviceIdType.MESH,
         )
 
-    def gather_copy(i):
-        k, q, dev = far(i)
-        rows = out_ref.at[pl.ds(pl.multiple_of(core * 512 + chip * 8, 8), 8)]
-        return pltpu.make_async_remote_copy(
-            src_ref=rows, dst_ref=rows, send_sem=gsem.at[k], recv_sem=grsem.at[k],
-            device_id=(dev,), device_id_type=pl.DeviceIdType.MESH,
-        )
-
-    def start_all(make):
-        def one(i, c):
-            make(i).start()
-            return c
-        lax.fori_loop(0, CHIPS - 1, one, 0)
-
-    def wait_all(make):
-        def one(i, c):
-            make(i).wait()
-            return c
-        lax.fori_loop(0, CHIPS - 1, one, 0)
-
-    start_all(scatter_copy)
+    scatters = [far_copy(dz, dr, False) for dz, dr in shifts]
+    for c in scatters:
+        c.start()
     small_end(cs, sml, smlr, 3)
-    wait_all(scatter_copy)
-    total = a1[rows_of(chip), :]
-    for k in range(CHIPS - 1):
-        total = total + rx[k]
-    out_ref[pl.ds(pl.multiple_of(core * 512 + chip * 8, 8), 8), :] = total
-    start_all(gather_copy)
-    wait_all(gather_copy)
-    half = out_ref.at[mine]
-    last = copy(half, half, twin)
+    for c in scatters:
+        c.wait()
+    total = [a1[rows_of(chip), :]] + [rx[k] for k in range(CHIPS - 1)]
+    while len(total) > 1:
+        total = [total[k] + total[k + 1] for k in range(0, len(total), 2)]
+    out_ref[mine8, :] = total[0]
+    gathers = {(dz, dr): far_copy(dz, dr, True) for dz, dr in shifts}
+    for c in gathers.values():
+        c.start()
+    last = []
+    for dz in (0, 1, 3, 2):
+        for dr in range(16):
+            if dz + dr > 0:
+                gathers[dz, dr].wait()
+        plane = pl.ds(pl.multiple_of(core * 512 + lax.rem(cz - dz + 4, 4) * 128, 128), 128)
+        last.append(copy(out_ref.at[plane], out_ref.at[plane], twin))
     loss_ref[...] = sml[24:25, 0:1] / count
     two_ref[...] = sml[0:19, :]
-    last.wait()
+    for c in last:
+        c.wait()
 
 
 def step(x, w_one, w_two, send_rows, src, dst, w, labels, mask):
     ma, mb = build(src, dst, w)
     vmem = pl.BlockSpec(memory_space=pltpu.VMEM)
-    n_sem = 30
+    n_sem = 36
     V = pltpu.VMEM
     loss, one, two = pl.pallas_call(
         step_kernel,
@@ -390,9 +393,9 @@
             V((2, HID, HALO), BF16), V((HID, HALO), BF16), V((HID, HALO), BF16),
             V((2, PADC, HALO), BF16), V((PADC, HALO), BF16), V((PADC, HALO), BF16),
             V((2, PADC, HALO), F32), V((PADC, HALO), F32), V((PADC, HALO), F32),
-            V((2, HID, HALO), F32), V((HID, HALO), F32), V((HID, HALO), F32),
+            V((2, 2, HID, QTR), F32), V((2, HID, QTR), F32), V((2, HID, QTR), F32),
             V((HID, NODES), F32), V((HID, NODES), BF16),
-            V((1024, HID), F32), V((512, HID), F32), V((512, HID), F32),
+            V((512, HID), F32), V((512, HID), F32), V((512, HID), F32),
             V((CHIPS - 1, 8, HID), F32),
             V((8, 128), F32), V((4, 4, 8, 128), F32), V((PADC, 128), F32), V((4, 4, PADC, 128), F32),
             V((HID, NODES), F32), V((HID, NODES), F32), V((HID, HID), F32),

time: 89.7 us -> 87 us (0.970)
  Pallas kernels: 85.7 us -> 83 us
    pallas_call x1, Pallas kernels: 67.8 us -> 65.3 us  [step(): pl.pallas_call(step_kernel, out_shape=[jax.ShapeDtypeStruct((1, 1), F32),...]
where the time goes in v4:
time: 87 us; the launch traced here: 86.9 us
  Pallas kernels  83 us (95%)
  between operations  2.43 us (3%)
  local copies, waits for them, and re-layouts  1.42 us (2%)
    pallas_call x1, Pallas kernels, step(): pl.pallas_call(step_kernel, out_shape=[jax.ShapeDtypeStruct((1, 1), F32),...  65.3 us
    pallas_call x1, Pallas kernels, build(): pl.pallas_call(build_kernel, out_shape=[o] * 2, in_specs=[H] * 3, out_spe...  17.7 us

profile of v4, /device:TPU:1, one launch (start us, length us, event | category | flops | bytes accessed | tf_op | source)
XLA Modules:
  0.0 86.9 jit_solution(17823828963676889079)
XLA Ops:
  0.6 0.0 copy-start
  0.6 0.0 copy-start.1
  0.7 0.0 copy-start.2
  0.7 0.0 copy-start.3
  0.7 0.0 copy-start.4
  0.7 0.0 copy-start.5
  0.7 17.7 %build.1 = (f32[16392,128]{1,0:T(8,128)S(1)}, f32[16392,128]{1,0:T(8,128)S(1)}) custom-call(s32[128,128]{1,0:T(8,128)} %bitcast.12, s32[128,128]{1,0:T(8,128)} %bitcast.13, f32[128,128]{1,0:T(8,128)} %bitcast.14), custom_call_target="tpu_custom_call" | custom-call | flops 10000000000 | bytes 80000000 | tf_op jit(solution)/shard_map/build/pallas_call | solution.py:139
  18.4 0.0 copy-done
  18.4 0.0 copy-done.1
  18.4 0.0 copy-done.2
  18.4 0.0 copy-done.3
  18.4 0.0 copy-done.4
  18.4 0.0 copy-done.5
  18.4 65.3 %step.1 = (f32[1,1]{1,0:T(1,128)}, f32[1024,128]{1,0:T(8,128)S(1)}, f32[19,128]{1,0:T(8,128)S(1)}) custom-call(bf16[1024,1024]{1,0:T(8,128)(2,1)S(1)} %copy-done, f32[1024,128]{1,0:T(8,128)S(1)} %copy-done.1, f32[19,128]{1,0:T(8,128)S(1)} %bitcast.8, s32[2,512]{1,0:T(2,128)S(1)} %copy-done.3, f32[16392,128]{1,0:T(8,128)S(1)} %get-tuple-element.8.ma_ref, ...), custom_call_target="tpu_custom_call" | custom-call | tf_op jit(solution)/shard_map/step/pallas_call | solution.py:382
  84.3 0.8 copy.16
  85.1 0.6 copy.17
Async XLA Ops:
  0.6 17.7 %copy-start = (bf16[1024,1024]{1,0:T(8,128)(2,1)S(1)}, bf16[1024,1024]{1,0:T(8,128)(2,1)}, u32[]{:S(2)}) copy-start(bf16[1024,1024]{1,0:T(8,128)(2,1)} %x_ref.1) | copy-start | bytes 6291460
  0.6 17.7 %copy-start.1 = (f32[1024,128]{1,0:T(8,128)S(1)}, f32[1024,128]{1,0:T(8,128)}, u32[]{:S(2)}) copy-start(f32[1024,128]{1,0:T(8,128)} %w1_ref.1) | copy-start | bytes 1572868
  0.7 17.7 %copy-start.2 = (f32[128,19]{0,1:T(8,128)S(1)}, f32[128,19]{0,1:T(8,128)}, u32[]{:S(2)}) copy-start(f32[128,19]{0,1:T(8,128)} %param.11) | copy-start | bytes 29188
  0.7 17.7 %copy-start.3 = (s32[2,512]{1,0:T(2,128)S(1)}, s32[2,512]{1,0:T(2,128)}, u32[]{:S(2)}) copy-start(s32[2,512]{1,0:T(2,128)} %send_ref.1) | copy-start | bytes 12292
  0.7 17.7 %copy-start.4 = (s32[1024]{0:T(1024)S(1)}, s32[1024]{0:T(1024)}, u32[]{:S(2)}) copy-start(s32[1024]{0:T(1024)} %param.16) | copy-start | bytes 12292
  0.7 17.7 %copy-start.5 = (s32[1024]{0:T(1024)S(1)}, s32[1024]{0:T(1024)}, u32[]{:S(2)}) copy-start(s32[1024]{0:T(1024)} %param.17) | copy-start | bytes 12292

commit v5 on v4

--- a/solution.py
+++ b/solution.py
@@ -144,9 +144,9 @@
 
 def step_kernel(
     x_ref, w1_ref, w2_ref, send_ref, ma_ref, mb_ref, lab_ref, mask_ref,
-    loss_ref, out_ref, two_ref,
+    out_ref, small_ref,
     s0_ref, s1_ref, sb1, hp1, hn1, sb2, hp2, hn2, gb2, ra2, rb2, gb1, ra1, rb1,
-    y_ref, hid_ref, part, rc, a1, rx, cnt, cntr, sml, smlr, own_ref, dy_ref, w2p, bh_ref, bm_ref, bl_ref, ssem, rsem, fsem, frsem, gsem, grsem,
+    y_ref, hid_ref, part, rc, a1, rx, cnt, cntr, sml, smlr, own_ref, dy_ref, w2p, bh_ref, bm_ref, bl_ref, r0_ref, r1_ref, ssem, rsem, fsem, frsem, gsem, grsem,
 ):
     me = lax.axis_index(AXIS)
     num = 128
@@ -236,6 +236,10 @@
     lax.fori_loop(0, NODES // 128, split_rows, 0)
     y_ref[...] = agg(t1, 0, NODES)
     lax.fori_loop(NODES // 128, EXT // 128, split_rows, 0)
+    column = lax.broadcasted_iota(jnp.int32, (HALO, NODES), 1).astype(F32)
+    for k, r_ref in ((0, r0_ref), (1, r1_ref)):
+        ids = jnp.broadcast_to(send_ref[k:k + 1, :].astype(F32), (8, HALO)).T[:, 0:1]
+        r_ref[...] = jnp.where(column == ids, 1.0, 0.0).astype(BF16)
     small_end(cc, cnt, cntr, 0)
     cc = small_start(cnt, cntr, 1)
     c_p.wait()
@@ -279,9 +283,9 @@
         rl = dot_t(dh, bl_ref[lo:hi, :])
         return rh[0:n] + ((rh[n:2 * n] + rm[0:n]) + (rh[2 * n:3 * n] + (rm[n:2 * n] + rl)))
 
-    def returned(r, s_ref):
+    def returned(r, s_rows):
         n = r.shape[0]
-        t = dot_t(jnp.concatenate(split3(r), axis=0), s_ref[...])
+        t = dot_n(jnp.concatenate(split3(r), axis=0), s_rows)
         return t[0:n] + (t[n:2 * n] + t[2 * n:3 * n])
 
     gb2[0] = agg_back(dz, NODES, NODES + HALO)
@@ -291,7 +295,7 @@
     own = agg_back(dz, 0, NODES)
     c_p.wait()
     c_n.wait()
-    dt2 = (own + (returned(ra2[...], s1_ref) + returned(rb2[...], s0_ref))).astype(BF16)
+    dt2 = (own + (returned(ra2[...], r1_ref[...]) + returned(rb2[...], r0_ref[...]))).astype(BF16)
     g2 = dot_t(dt2, hid_ref[...])
     sml[...] = g2
     sml[24:32, :] = jnp.broadcast_to(loss, (8, 128))
@@ -310,10 +314,10 @@
     small_end(cs, sml, smlr, 1)
     cs = small_start(sml, smlr, 2)
     for h in range(2):
-        cols = pl.ds(h * QTR, QTR)
+        slots = pl.ds(h * QTR, QTR)
         back[2 * h].wait()
         back[2 * h + 1].wait()
-        own_ref[...] += returned(ra1[h], s1_ref.at[:, cols]) + returned(rb1[h], s0_ref.at[:, cols])
+        own_ref[...] += returned(ra1[h], r1_ref[slots, :]) + returned(rb1[h], r0_ref[slots, :])
     dt1 = own_ref[...].astype(BF16)
 
     mine = pl.ds(pl.multiple_of(core * 512, 512), 512)
@@ -368,10 +372,37 @@
                 gathers[dz, dr].wait()
         plane = pl.ds(pl.multiple_of(core * 512 + lax.rem(cz - dz + 4, 4) * 128, 128), 128)
         last.append(copy(out_ref.at[plane], out_ref.at[plane], twin))
-    loss_ref[...] = sml[24:25, 0:1] / count
-    two_ref[...] = sml[0:19, :]
+    small_ref[...] = sml[...]
+    small_ref[24:32, :] = sml[24:32, :] / count
     for c in last:
         c.wait()
+
+
+def finish_kernel(one_in, small_in, loss_ref, one_ref, two_ref, two_v, sem):
+    one = pltpu.make_async_copy(one_in, one_ref, sem.at[0])
+    one.start()
+    two_v[...] = small_in[0:19, :]
+    two = pltpu.make_async_copy(two_v, two_ref, sem.at[1])
+    two.start()
+    loss_ref[0, 0] = jnp.max(small_in[24:25, :])
+    one.wait()
+    two.wait()
+
+
+def finish(one, small):
+    vmem = pl.BlockSpec(memory_space=pltpu.VMEM)
+    hbm = pl.BlockSpec(memory_space=pltpu.HBM)
+    return pl.pallas_call(
+        finish_kernel,
+        out_shape=[
+            jax.ShapeDtypeStruct((1, 1), F32), jax.ShapeDtypeStruct(one.shape, F32), jax.ShapeDtypeStruct((19, HID), F32),
+        ],
+        in_specs=[vmem] * 2,
+        out_specs=[pl.BlockSpec(memory_space=pltpu.SMEM), hbm, hbm],
+        scratch_shapes=[pltpu.VMEM((19, HID), F32), pltpu.SemaphoreType.DMA((2,))],
+        name="finish",
+        compiler_params=pltpu.CompilerParams(vmem_limit_bytes=4 * 1024 * 1024),
+    )(one, small)
 
 
 def step(x, w_one, w_two, send_rows, src, dst, w, labels, mask):
@@ -379,15 +410,14 @@
     vmem = pl.BlockSpec(memory_space=pltpu.VMEM)
     n_sem = 36
     V = pltpu.VMEM
-    loss, one, two = pl.pallas_call(
+    one, small = pl.pallas_call(
         step_kernel,
         out_shape=[
-            jax.ShapeDtypeStruct((1, 1), F32),
             jax.ShapeDtypeStruct((1024, HID), F32),
-            jax.ShapeDtypeStruct((19, HID), F32),
+            jax.ShapeDtypeStruct((PADC, HID), F32),
         ],
         in_specs=[vmem] * 8,
-        out_specs=[vmem] * 3,
+        out_specs=[vmem] * 2,
         scratch_shapes=[
             V((NODES, HALO), BF16), V((NODES, HALO), BF16),
             V((2, HID, HALO), BF16), V((HID, HALO), BF16), V((HID, HALO), BF16),
@@ -400,6 +430,7 @@
             V((8, 128), F32), V((4, 4, 8, 128), F32), V((PADC, 128), F32), V((4, 4, PADC, 128), F32),
             V((HID, NODES), F32), V((HID, NODES), F32), V((HID, HID), F32),
             V((EXT, NODES), BF16), V((EXT, NODES), BF16), V((EXT, NODES), BF16),
+            V((HALO, NODES), BF16), V((HALO, NODES), BF16),
             pltpu.SemaphoreType.DMA((n_sem,)), pltpu.SemaphoreType.DMA((n_sem,)),
             *[pltpu.SemaphoreType.DMA((CHIPS - 1,))] * 4,
         ],
@@ -408,6 +439,7 @@
             collective_id=0, has_side_effects=True, vmem_limit_bytes=31 * 1024 * 1024
         ),
     )(x, w_one, w_two.T, send_rows, ma, mb, labels.reshape(1, NODES), mask.reshape(1, NODES))
+    loss, one, two = finish(one, small)
     return loss.reshape(()), one, two.T
 
 

time: 87 us -> 84.3 us (0.969)
  between operations: 2.43 us -> 0.9 us
  local copies, waits for them, and re-layouts: 1.42 us -> 0.03 us
    unnamed x14 -> x12, local copies, waits for them, and re-layouts: 1.42 us -> 0.03 us
    pallas_call x1 -> x2, Pallas kernels: 65.3 us -> 65.7 us  [the longest x1 64.3 us: step(): pl.pallas_call(step_kernel, out_shape=[jax.ShapeDtypeStruct((1024, HID),...]
where the time goes in v5:
time: 84.3 us; the launch traced here: 84.2 us
  Pallas kernels  83.3 us (99%)
  between operations  0.9 us (1%)
    pallas_call x1, Pallas kernels, step(): pl.pallas_call(step_kernel, out_shape=[jax.ShapeDtypeStruct((1024, HID),...  64.3 us
    pallas_call x1, Pallas kernels, build(): pl.pallas_call(build_kernel, out_shape=[o] * 2, in_specs=[H] * 3, out_spe...  17.6 us

profile of v5, /device:TPU:1, one launch (start us, length us, event | category | flops | bytes accessed | tf_op | source)
XLA Modules:
  0.0 84.2 jit_solution(17977909130391864441)
XLA Ops:
  0.6 0.0 copy-start
  0.6 0.0 copy-start.1
  0.7 0.0 copy-start.2
  0.7 0.0 copy-start.3
  0.7 0.0 copy-start.4
  0.7 0.0 copy-start.5
  0.7 17.6 %build.1 = (f32[16392,128]{1,0:T(8,128)S(1)}, f32[16392,128]{1,0:T(8,128)S(1)}) custom-call(s32[128,128]{1,0:T(8,128)} %bitcast.11, s32[128,128]{1,0:T(8,128)} %bitcast.12, f32[128,128]{1,0:T(8,128)} %bitcast.13), custom_call_target="tpu_custom_call" | custom-call | flops 10000000000 | bytes 80000000 | tf_op jit(solution)/shard_map/build/pallas_call | solution.py:139
  18.3 0.0 copy-done
  18.3 0.0 copy-done.1
  18.3 0.0 copy-done.2
  18.4 0.0 copy-done.3
  18.4 0.0 copy-done.4
  18.4 0.0 copy-done.5
  18.4 64.3 %step.1 = (f32[1024,128]{1,0:T(8,128)S(1)}, f32[32,128]{1,0:T(8,128)S(1)}) custom-call(bf16[1024,1024]{1,0:T(8,128)(2,1)S(1)} %copy-done, f32[1024,128]{1,0:T(8,128)S(1)} %copy-done.1, f32[19,128]{1,0:T(8,128)S(1)} %bitcast.8, s32[2,512]{1,0:T(2,128)S(1)} %copy-done.3, f32[16392,128]{1,0:T(8,128)S(1)} %get-tuple-element.10.ma_ref, ...), custom_call_target="tpu_custom_call" | custom-call | tf_op jit(solution)/shard_map/step/pallas_call | solution.py:413
  82.7 1.3 %finish.1 = (f32[1,1]{1,0:T(1,128)}, f32[1024,128]{1,0:T(8,128)}, f32[19,128]{1,0:T(8,128)}) custom-call(f32[1024,128]{1,0:T(8,128)S(1)} %get-tuple-element.12.one_in, f32[32,128]{1,0:T(8,128)S(1)} %get-tuple-element.13.small_in), custom_call_target="tpu_custom_call" | custom-call | tf_op jit(solution)/shard_map/finish/pallas_call | solution.py:395
Async XLA Ops:
  0.6 17.7 %copy-start = (bf16[1024,1024]{1,0:T(8,128)(2,1)S(1)}, bf16[1024,1024]{1,0:T(8,128)(2,1)}, u32[]{:S(2)}) copy-start(bf16[1024,1024]{1,0:T(8,128)(2,1)} %x_ref.1) | copy-start | bytes 6291460
  0.6 17.7 %copy-start.1 = (f32[1024,128]{1,0:T(8,128)S(1)}, f32[1024,128]{1,0:T(8,128)}, u32[]{:S(2)}) copy-start(f32[1024,128]{1,0:T(8,128)} %w1_ref.1) | copy-start | bytes 1572868
  0.7 17.7 %copy-start.2 = (f32[128,19]{0,1:T(8,128)S(1)}, f32[128,19]{0,1:T(8,128)}, u32[]{:S(2)}) copy-start(f32[128,19]{0,1:T(8,128)} %param.11) | copy-start | bytes 29188
  0.7 17.7 %copy-start.3 = (s32[2,512]{1,0:T(2,128)S(1)}, s32[2,512]{1,0:T(2,128)}, u32[]{:S(2)}) copy-start(s32[2,512]{1,0:T(2,128)} %send_ref.1) | copy-start | bytes 12292
  0.7 17.7 %copy-start.4 = (s32[1024]{0:T(1024)S(1)}, s32[1024]{0:T(1024)}, u32[]{:S(2)}) copy-start(s32[1024]{0:T(1024)} %param.16) | copy-start | bytes 12292
  0.7 17.7 %copy-start.5 = (s32[1024]{0:T(1024)S(1)}, s32[1024]{0:T(1024)}, u32[]{:S(2)}) copy-start(s32[1024]{0:T(1024)} %param.17) | copy-start | bytes 12292

commit v6 on v5

--- a/solution.py
+++ b/solution.py
@@ -154,8 +154,7 @@
     cx = lax.rem(me // 2, 4)
     cy = lax.rem(me // 8, 4)
     cz = me // 32
-    nxt = lax.rem(me + 1, num)
-    prv = lax.rem(me + num - 1, num)
+    away = lax.rem(me + num - 1 + 2 * core, num)
     twin = me + 1 - 2 * core
     dims = ((cx, 2), (cy, 8), (cz, 32))
 
@@ -165,7 +164,7 @@
         return p, me + (p - c) * stride
 
     barrier = pltpu.get_barrier_semaphore()
-    targets = [nxt, prv, twin] + [peer(k, d)[1] for k in range(3) for d in (1, 2, 3)]
+    targets = [away, twin] + [peer(k, d)[1] for k in range(3) for d in (1, 2, 3)]
     for t in targets:
         pl.semaphore_signal(barrier, inc=1, device_id=(t,), device_id_type=pl.DeviceIdType.MESH)
 
@@ -205,16 +204,16 @@
     w2n = w2p[...].T.astype(BF16)[:, 0:PADC]
 
     node = lax.broadcasted_iota(jnp.int32, (NODES, HALO), 0)
-    s0_ref[...] = jnp.where(node == send_ref[0:1, :], 1.0, 0.0).astype(BF16)
-    s1_ref[...] = jnp.where(node == send_ref[1:2, :], 1.0, 0.0).astype(BF16)
+    s0_ref[...] = jnp.where(node == send_ref[pl.ds(1 - core, 1), :], 1.0, 0.0).astype(BF16)
+    s1_ref[...] = jnp.where(node == send_ref[pl.ds(core, 1), :], 1.0, 0.0).astype(BF16)
 
     t1 = dot_n(x_ref[...], w1_ref[...].astype(BF16))
     t1 = t1.T.astype(BF16)
     sb1[1] = dot_n(t1, s1_ref[...]).astype(BF16)
+    pl.semaphore_wait(barrier, len(targets))
+    c_p = copy(sb1.at[1], hp1, away)
     sb1[0] = dot_n(t1, s0_ref[...]).astype(BF16)
-    pl.semaphore_wait(barrier, len(targets))
-    c_p = copy(sb1.at[1], hp1, nxt)
-    c_n = copy(sb1.at[0], hn1, prv)
+    c_n = copy(sb1.at[0], hn1, twin)
     cc = small_start(cnt, cntr, 0)
 
     def agg(e, lo, hi):
@@ -222,29 +221,34 @@
         acc = acc + dot_n(e, bm_ref[lo:hi, :])
         return acc + dot_n(e, bh_ref[lo:hi, :])
 
-    def split_rows(i, c):
-        rows = pl.ds(pl.multiple_of(i * 128, 128), 128)
-        for j in range(NODES // 128):
-            part_rows = pl.ds(pl.multiple_of(j * EXT + i * 128, 128), 128)
-            h, m, l = split3(ma_ref[part_rows, :] + mb_ref[part_rows, :])
-            cols = pl.ds(j * 128, 128)
-            bh_ref[rows, cols] = h
-            bm_ref[rows, cols] = m
-            bl_ref[rows, cols] = l
-        return c
-
-    lax.fori_loop(0, NODES // 128, split_rows, 0)
+    def split_block(first, source, blocks):
+        def one(i, c):
+            rows = pl.ds(pl.multiple_of((first + i) * 128, 128), 128)
+            for j in range(NODES // 128):
+                from_rows = pl.ds(pl.multiple_of(j * EXT + (source + i) * 128, 128), 128)
+                h, m, l = split3(ma_ref[from_rows, :] + mb_ref[from_rows, :])
+                cols = pl.ds(j * 128, 128)
+                bh_ref[rows, cols] = h
+                bm_ref[rows, cols] = m
+                bl_ref[rows, cols] = l
+            return c
+
+        lax.fori_loop(0, blocks, one, 0)
+
+    split_block(0, 0, 8)
     y_ref[...] = agg(t1, 0, NODES)
-    lax.fori_loop(NODES // 128, EXT // 128, split_rows, 0)
+    split_block(12, 12 - 4 * core, 4)
+    split_block(8, 8 + 4 * core, 4)
     column = lax.broadcasted_iota(jnp.int32, (HALO, NODES), 1).astype(F32)
-    for k, r_ref in ((0, r0_ref), (1, r1_ref)):
-        ids = jnp.broadcast_to(send_ref[k:k + 1, :].astype(F32), (8, HALO)).T[:, 0:1]
+    for k, r_ref in ((1 - core, r0_ref), (core, r1_ref)):
+        ids = jnp.broadcast_to(send_ref[pl.ds(k, 1), :].astype(F32), (8, HALO)).T[:, 0:1]
         r_ref[...] = jnp.where(column == ids, 1.0, 0.0).astype(BF16)
     small_end(cc, cnt, cntr, 0)
     cc = small_start(cnt, cntr, 1)
+    c_n.wait()
+    y_ref[...] += agg(hn1[...], NODES + HALO, EXT)
     c_p.wait()
-    c_n.wait()
-    y = y_ref[...] + (agg(hp1[...], NODES, NODES + HALO) + agg(hn1[...], NODES + HALO, EXT))
+    y = y_ref[...] + agg(hp1[...], NODES, NODES + HALO)
     y_ref[...] = y
     small_end(cc, cnt, cntr, 1)
     cc = small_start(cnt, cntr, 2)
@@ -252,15 +256,16 @@
     hid_ref[...] = hid
     t2 = dot_n(w2t, hid).astype(BF16)
     sb2[1] = dot_n(t2, s1_ref[...]).astype(BF16)
+    c_p = copy(sb2.at[1], hp2, away)
     sb2[0] = dot_n(t2, s0_ref[...]).astype(BF16)
-    c_p = copy(sb2.at[1], hp2, nxt)
-    c_n = copy(sb2.at[0], hn2, prv)
+    c_n = copy(sb2.at[0], hn2, twin)
     z = agg(t2, 0, NODES)
     small_end(cc, cnt, cntr, 2)
     cc = small_start(cnt, cntr, 3)
+    c_n.wait()
+    z = z + agg(hn2[...], NODES + HALO, EXT)
     c_p.wait()
-    c_n.wait()
-    z = z + (agg(hp2[...], NODES, NODES + HALO) + agg(hn2[...], NODES + HALO, EXT))
+    z = z + agg(hp2[...], NODES, NODES + HALO)
     small_end(cc, cnt, cntr, 3)
     count = jnp.maximum(cnt[0:1, 0:1], 1.0)
 
@@ -289,13 +294,14 @@
         return t[0:n] + (t[n:2 * n] + t[2 * n:3 * n])
 
     gb2[0] = agg_back(dz, NODES, NODES + HALO)
-    c_p = copy(gb2.at[0], ra2, prv)
+    c_p = copy(gb2.at[0], ra2, away)
     gb2[1] = agg_back(dz, NODES + HALO, EXT)
-    c_n = copy(gb2.at[1], rb2, nxt)
+    c_n = copy(gb2.at[1], rb2, twin)
     own = agg_back(dz, 0, NODES)
+    c_n.wait()
+    own = own + returned(rb2[...], r0_ref[...])
     c_p.wait()
-    c_n.wait()
-    dt2 = (own + (returned(ra2[...], r1_ref[...]) + returned(rb2[...], r0_ref[...]))).astype(BF16)
+    dt2 = (own + returned(ra2[...], r1_ref[...])).astype(BF16)
     g2 = dot_t(dt2, hid_ref[...])
     sml[...] = g2
     sml[24:32, :] = jnp.broadcast_to(loss, (8, 128))
@@ -303,21 +309,20 @@
     dh = dot_n(w2n, dt2)
     dy_ref[...] = jnp.where(y_ref[...] > 0.0, dh, 0.0)
     back = []
-    for h in range(2):
-        gb1[0, h] = agg_back(dy_ref[...], NODES + h * QTR, NODES + (h + 1) * QTR)
-        back.append(copy(gb1.at[0, h], ra1.at[h], prv))
-        gb1[1, h] = agg_back(dy_ref[...], NODES + HALO + h * QTR, NODES + HALO + (h + 1) * QTR)
-        back.append(copy(gb1.at[1, h], rb1.at[h], nxt))
+    for side, land, dev in ((0, ra1, away), (1, rb1, twin)):
+        for h in range(2):
+            first = NODES + side * HALO + h * QTR
+            gb1[side, h] = agg_back(dy_ref[...], first, first + QTR)
+            back.append(copy(gb1.at[side, h], land.at[h], dev))
     small_end(cs, sml, smlr, 0)
     cs = small_start(sml, smlr, 1)
     own_ref[...] = agg_back(dy_ref[...], 0, NODES)
     small_end(cs, sml, smlr, 1)
     cs = small_start(sml, smlr, 2)
-    for h in range(2):
-        slots = pl.ds(h * QTR, QTR)
-        back[2 * h].wait()
-        back[2 * h + 1].wait()
-        own_ref[...] += returned(ra1[h], r1_ref[slots, :]) + returned(rb1[h], r0_ref[slots, :])
+    for side, land, rows_ref in ((1, rb1, r0_ref), (0, ra1, r1_ref)):
+        for h in range(2):
+            back[2 * side + h].wait()
+            own_ref[...] += returned(land[h], rows_ref[pl.ds(h * QTR, QTR), :])
     dt1 = own_ref[...].astype(BF16)
 
     mine = pl.ds(pl.multiple_of(core * 512, 512), 512)

time: 84.3 us -> 82.1 us (0.974)
  Pallas kernels: 83.3 us -> 81.1 us
    pallas_call x1, Pallas kernels: 64.3 us -> 62.1 us  [step(): pl.pallas_call(step_kernel, out_shape=[jax.ShapeDtypeStruct((1024, HID),...]
where the time goes in v6:
time: 82.1 us; the launch traced here: 82 us
  Pallas kernels  81.1 us (99%)
  between operations  0.9 us (1%)
    pallas_call x1, Pallas kernels, step(): pl.pallas_call(step_kernel, out_shape=[jax.ShapeDtypeStruct((1024, HID),...  62.1 us
    pallas_call x1, Pallas kernels, build(): pl.pallas_call(build_kernel, out_shape=[o] * 2, in_specs=[H] * 3, out_spe...  17.6 us

profile of v6, /device:TPU:1, one launch (start us, length us, event | category | flops | bytes accessed | tf_op | source)
XLA Modules:
  0.0 82.0 jit_solution(867230355860031310)
XLA Ops:
  0.6 0.0 copy-start
  0.6 0.0 copy-start.1
  0.7 0.0 copy-start.2
  0.7 0.0 copy-start.3
  0.7 0.0 copy-start.4
  0.7 0.0 copy-start.5
  0.7 17.6 %build.1 = (f32[16392,128]{1,0:T(8,128)S(1)}, f32[16392,128]{1,0:T(8,128)S(1)}) custom-call(s32[128,128]{1,0:T(8,128)} %bitcast.11, s32[128,128]{1,0:T(8,128)} %bitcast.12, f32[128,128]{1,0:T(8,128)} %bitcast.13), custom_call_target="tpu_custom_call" | custom-call | flops 10000000000 | bytes 80000000 | tf_op jit(solution)/shard_map/build/pallas_call | solution.py:139
  18.3 0.0 copy-done
  18.3 0.0 copy-done.1
  18.3 0.0 copy-done.2
  18.3 0.0 copy-done.3
  18.4 0.0 copy-done.4
  18.4 0.0 copy-done.5
  18.4 62.1 %step.1 = (f32[1024,128]{1,0:T(8,128)S(1)}, f32[32,128]{1,0:T(8,128)S(1)}) custom-call(bf16[1024,1024]{1,0:T(8,128)(2,1)S(1)} %copy-done, f32[1024,128]{1,0:T(8,128)S(1)} %copy-done.1, f32[19,128]{1,0:T(8,128)S(1)} %bitcast.8, s32[2,512]{1,0:T(2,128)S(1)} %copy-done.3, f32[16392,128]{1,0:T(8,128)S(1)} %get-tuple-element.10.ma_ref, ...), custom_call_target="tpu_custom_call" | custom-call | tf_op jit(solution)/shard_map/step/pallas_call | solution.py:418
  80.5 1.3 %finish.1 = (f32[1,1]{1,0:T(1,128)}, f32[1024,128]{1,0:T(8,128)}, f32[19,128]{1,0:T(8,128)}) custom-call(f32[1024,128]{1,0:T(8,128)S(1)} %get-tuple-element.12.one_in, f32[32,128]{1,0:T(8,128)S(1)} %get-tuple-element.13.small_in), custom_call_target="tpu_custom_call" | custom-call | tf_op jit(solution)/shard_map/finish/pallas_call | solution.py:400
Async XLA Ops:
  0.6 17.7 %copy-start = (bf16[1024,1024]{1,0:T(8,128)(2,1)S(1)}, bf16[1024,1024]{1,0:T(8,128)(2,1)}, u32[]{:S(2)}) copy-start(bf16[1024,1024]{1,0:T(8,128)(2,1)} %x_ref.1) | copy-start | bytes 6291460
  0.6 17.7 %copy-start.1 = (f32[1024,128]{1,0:T(8,128)S(1)}, f32[1024,128]{1,0:T(8,128)}, u32[]{:S(2)}) copy-start(f32[1024,128]{1,0:T(8,128)} %w1_ref.1) | copy-start | bytes 1572868
  0.7 17.7 %copy-start.2 = (f32[128,19]{0,1:T(8,128)S(1)}, f32[128,19]{0,1:T(8,128)}, u32[]{:S(2)}) copy-start(f32[128,19]{0,1:T(8,128)} %param.11) | copy-start | bytes 29188
  0.7 17.7 %copy-start.3 = (s32[2,512]{1,0:T(2,128)S(1)}, s32[2,512]{1,0:T(2,128)}, u32[]{:S(2)}) copy-start(s32[2,512]{1,0:T(2,128)} %send_ref.1) | copy-start | bytes 12292
  0.7 17.7 %copy-start.4 = (s32[1024]{0:T(1024)S(1)}, s32[1024]{0:T(1024)}, u32[]{:S(2)}) copy-start(s32[1024]{0:T(1024)} %param.16) | copy-start | bytes 12292
  0.7 17.7 %copy-start.5 = (s32[1024]{0:T(1024)S(1)}, s32[1024]{0:T(1024)}, u32[]{:S(2)}) copy-start(s32[1024]{0:T(1024)} %param.17) | copy-start | bytes 12292

commit v7 on v6

--- a/solution.py
+++ b/solution.py
@@ -145,8 +145,8 @@
 def step_kernel(
     x_ref, w1_ref, w2_ref, send_ref, ma_ref, mb_ref, lab_ref, mask_ref,
     out_ref, small_ref,
-    s0_ref, s1_ref, sb1, hp1, hn1, sb2, hp2, hn2, gb2, ra2, rb2, gb1, ra1, rb1,
-    y_ref, hid_ref, part, rc, a1, rx, cnt, cntr, sml, smlr, own_ref, dy_ref, w2p, bh_ref, bm_ref, bl_ref, r0_ref, r1_ref, ssem, rsem, fsem, frsem, gsem, grsem,
+    s0_ref, s1_ref, sb1, hp1, hn1, sb2, hp2, hn2, ga2, gb2, ra2, rb2, gb1, ra1, rb1,
+    y_ref, hid_ref, part, rc, a1, rx, cnt, cntr, sml, smlr, own_ref, dy_ref, w2p, bh_ref, bm_ref, bl_ref, r0_ref, r1_ref, ssem, rsem, fsem, frsem, gsem, grsem, bsem, brsem,
 ):
     me = lax.axis_index(AXIS)
     num = 128
@@ -293,15 +293,19 @@
         t = dot_n(jnp.concatenate(split3(r), axis=0), s_rows)
         return t[0:n] + (t[n:2 * n] + t[2 * n:3 * n])
 
-    gb2[0] = agg_back(dz, NODES, NODES + HALO)
-    c_p = copy(gb2.at[0], ra2, away)
-    gb2[1] = agg_back(dz, NODES + HALO, EXT)
-    c_n = copy(gb2.at[1], rb2, twin)
+    c_p = []
+    for h in range(2):
+        ga2[h] = agg_back(dz, NODES + h * QTR, NODES + (h + 1) * QTR)
+        c_p.append(copy(ga2.at[h], ra2.at[h], away))
+    gb2[...] = agg_back(dz, NODES + HALO, EXT)
+    c_n = copy(gb2, rb2, twin)
     own = agg_back(dz, 0, NODES)
     c_n.wait()
     own = own + returned(rb2[...], r0_ref[...])
-    c_p.wait()
-    dt2 = (own + returned(ra2[...], r1_ref[...])).astype(BF16)
+    for h in range(2):
+        c_p[h].wait()
+        own = own + returned(ra2[h], r1_ref[pl.ds(h * QTR, QTR), :])
+    dt2 = own.astype(BF16)
     g2 = dot_t(dt2, hid_ref[...])
     sml[...] = g2
     sml[24:32, :] = jnp.broadcast_to(loss, (8, 128))
@@ -368,18 +372,27 @@
         total = [total[k] + total[k + 1] for k in range(0, len(total), 2)]
     out_ref[mine8, :] = total[0]
     gathers = {(dz, dr): far_copy(dz, dr, True) for dz, dr in shifts}
-    for c in gathers.values():
+    both = []
+    for dr in range(16):
+        _, q, _ = far(2, dr)
+        both.append(pltpu.make_async_remote_copy(
+            src_ref=out_ref.at[mine8], dst_ref=out_ref.at[mine8], send_sem=bsem.at[dr], recv_sem=brsem.at[dr],
+            device_id=(q * 2 + 1 - core,), device_id_type=pl.DeviceIdType.MESH,
+        ))
+    for c in [gathers[2, dr] for dr in range(16)] + both + [c for (dz, _), c in gathers.items() if dz != 2]:
         c.start()
     last = []
     for dz in (0, 1, 3, 2):
         for dr in range(16):
             if dz + dr > 0:
                 gathers[dz, dr].wait()
+        if dz == 2:
+            continue
         plane = pl.ds(pl.multiple_of(core * 512 + lax.rem(cz - dz + 4, 4) * 128, 128), 128)
         last.append(copy(out_ref.at[plane], out_ref.at[plane], twin))
     small_ref[...] = sml[...]
     small_ref[24:32, :] = sml[24:32, :] / count
-    for c in last:
+    for c in both + last:
         c.wait()
 
 
@@ -427,7 +440,7 @@
             V((NODES, HALO), BF16), V((NODES, HALO), BF16),
             V((2, HID, HALO), BF16), V((HID, HALO), BF16), V((HID, HALO), BF16),
             V((2, PADC, HALO), BF16), V((PADC, HALO), BF16), V((PADC, HALO), BF16),
-            V((2, PADC, HALO), F32), V((PADC, HALO), F32), V((PADC, HALO), F32),
+            V((2, PADC, QTR), F32), V((PADC, HALO), F32), V((2, PADC, QTR), F32), V((PADC, HALO), F32),
             V((2, 2, HID, QTR), F32), V((2, HID, QTR), F32), V((2, HID, QTR), F32),
             V((HID, NODES), F32), V((HID, NODES), BF16),
             V((512, HID), F32), V((512, HID), F32), V((512, HID), F32),
@@ -438,6 +451,7 @@
             V((HALO, NODES), BF16), V((HALO, NODES), BF16),
             pltpu.SemaphoreType.DMA((n_sem,)), pltpu.SemaphoreType.DMA((n_sem,)),
             *[pltpu.SemaphoreType.DMA((CHIPS - 1,))] * 4,
+            *[pltpu.SemaphoreType.DMA((16,))] * 2,
         ],
         name="step",
         compiler_params=pltpu.CompilerParams(

time: 82.1 us -> 82.8 us (level)
  no operation moved by 1% of the time
where the time goes in v7:
time: 82.8 us; the launch traced here: 82.7 us
  Pallas kernels  81.7 us (99%)
  between operations  0.9 us (1%)
    pallas_call x1, Pallas kernels, step(): pl.pallas_call(step_kernel, out_shape=[jax.ShapeDtypeStruct((1024, HID),...  62.8 us
    pallas_call x1, Pallas kernels, build(): pl.pallas_call(build_kernel, out_shape=[o] * 2, in_specs=[H] * 3, out_spe...  17.6 us

profile of v7, /device:TPU:1, one launch (start us, length us, event | category | flops | bytes accessed | tf_op | source)
XLA Modules:
  0.0 82.7 jit_solution(6879448326528074002)
XLA Ops:
  0.6 0.0 copy-start
  0.6 0.0 copy-start.1
  0.7 0.0 copy-start.2
  0.7 0.0 copy-start.3
  0.7 0.0 copy-start.4
  0.7 0.0 copy-start.5
  0.7 17.6 %build.1 = (f32[16392,128]{1,0:T(8,128)S(1)}, f32[16392,128]{1,0:T(8,128)S(1)}) custom-call(s32[128,128]{1,0:T(8,128)} %bitcast.11, s32[128,128]{1,0:T(8,128)} %bitcast.12, f32[128,128]{1,0:T(8,128)} %bitcast.13), custom_call_target="tpu_custom_call" | custom-call | flops 10000000000 | bytes 80000000 | tf_op jit(solution)/shard_map/build/pallas_call | solution.py:139
  18.3 0.0 copy-done
  18.4 0.0 copy-done.1
  18.4 0.0 copy-done.2
  18.4 0.0 copy-done.3
  18.4 0.0 copy-done.4
  18.4 0.0 copy-done.5
  18.4 62.8 %step.1 = (f32[1024,128]{1,0:T(8,128)S(1)}, f32[32,128]{1,0:T(8,128)S(1)}) custom-call(bf16[1024,1024]{1,0:T(8,128)(2,1)S(1)} %copy-done, f32[1024,128]{1,0:T(8,128)S(1)} %copy-done.1, f32[19,128]{1,0:T(8,128)S(1)} %bitcast.8, s32[2,512]{1,0:T(2,128)S(1)} %copy-done.3, f32[16392,128]{1,0:T(8,128)S(1)} %get-tuple-element.10.ma_ref, ...), custom_call_target="tpu_custom_call" | custom-call | tf_op jit(solution)/shard_map/step/pallas_call | solution.py:431
  81.2 1.3 %finish.1 = (f32[1,1]{1,0:T(1,128)}, f32[1024,128]{1,0:T(8,128)}, f32[19,128]{1,0:T(8,128)}) custom-call(f32[1024,128]{1,0:T(8,128)S(1)} %get-tuple-element.12.one_in, f32[32,128]{1,0:T(8,128)S(1)} %get-tuple-element.13.small_in), custom_call_target="tpu_custom_call" | custom-call | tf_op jit(solution)/shard_map/finish/pallas_call | solution.py:413
Async XLA Ops:
  0.6 17.7 %copy-start = (bf16[1024,1024]{1,0:T(8,128)(2,1)S(1)}, bf16[1024,1024]{1,0:T(8,128)(2,1)}, u32[]{:S(2)}) copy-start(bf16[1024,1024]{1,0:T(8,128)(2,1)} %x_ref.1) | copy-start | bytes 6291460
  0.6 17.7 %copy-start.1 = (f32[1024,128]{1,0:T(8,128)S(1)}, f32[1024,128]{1,0:T(8,128)}, u32[]{:S(2)}) copy-start(f32[1024,128]{1,0:T(8,128)} %w1_ref.1) | copy-start | bytes 1572868
  0.7 17.7 %copy-start.2 = (f32[128,19]{0,1:T(8,128)S(1)}, f32[128,19]{0,1:T(8,128)}, u32[]{:S(2)}) copy-start(f32[128,19]{0,1:T(8,128)} %param.11) | copy-start | bytes 29188
  0.7 17.7 %copy-start.3 = (s32[2,512]{1,0:T(2,128)S(1)}, s32[2,512]{1,0:T(2,128)}, u32[]{:S(2)}) copy-start(s32[2,512]{1,0:T(2,128)} %send_ref.1) | copy-start | bytes 12292
  0.7 17.7 %copy-start.4 = (s32[1024]{0:T(1024)S(1)}, s32[1024]{0:T(1024)}, u32[]{:S(2)}) copy-start(s32[1024]{0:T(1024)} %param.16) | copy-start | bytes 12292
  0.7 17.7 %copy-start.5 = (s32[1024]{0:T(1024)S(1)}, s32[1024]{0:T(1024)}, u32[]{:S(2)}) copy-start(s32[1024]{0:T(1024)} %param.17) | copy-start | bytes 12292

commit v8 on v7

--- a/solution.py
+++ b/solution.py
@@ -146,7 +146,7 @@
     x_ref, w1_ref, w2_ref, send_ref, ma_ref, mb_ref, lab_ref, mask_ref,
     out_ref, small_ref,
     s0_ref, s1_ref, sb1, hp1, hn1, sb2, hp2, hn2, ga2, gb2, ra2, rb2, gb1, ra1, rb1,
-    y_ref, hid_ref, part, rc, a1, rx, cnt, cntr, sml, smlr, own_ref, dy_ref, w2p, bh_ref, bm_ref, bl_ref, r0_ref, r1_ref, ssem, rsem, fsem, frsem, gsem, grsem, bsem, brsem,
+    y_ref, hid_ref, part, rc, a1, rx, cnt, cntr, sml, smlr, own_ref, dy_ref, w2p, bh_ref, bm_ref, bl_ref, r0_ref, r1_ref, ssem, rsem, fsem, frsem, gsem, grsem,
 ):
     me = lax.axis_index(AXIS)
     num = 128
@@ -274,11 +274,13 @@
     mask = mask_ref[...].astype(F32)
     zm = jnp.where(real, z, -jnp.inf)
     top = jnp.max(zm, axis=0, keepdims=True)
-    norm = jnp.log(jnp.sum(jnp.where(real, jnp.exp(z - top), 0.0), axis=0, keepdims=True)) + top
+    grown = jnp.where(real, jnp.exp(zm - top), 0.0)
+    weight = jnp.sum(grown, axis=0, keepdims=True)
+    norm = jnp.log(weight) + top
     hot = (cls == lab_ref[...]).astype(F32)
     picked = jnp.sum(z * hot, axis=0, keepdims=True)
     loss = jnp.sum(mask * (norm - picked), axis=1, keepdims=True)
-    dz = (jnp.where(real, jnp.exp(z - norm), 0.0) - hot) * (mask / count)
+    dz = (grown / weight - hot) * (mask / count)
 
     def agg_back(d, lo, hi):
         n = d.shape[0]
@@ -372,27 +374,18 @@
         total = [total[k] + total[k + 1] for k in range(0, len(total), 2)]
     out_ref[mine8, :] = total[0]
     gathers = {(dz, dr): far_copy(dz, dr, True) for dz, dr in shifts}
-    both = []
-    for dr in range(16):
-        _, q, _ = far(2, dr)
-        both.append(pltpu.make_async_remote_copy(
-            src_ref=out_ref.at[mine8], dst_ref=out_ref.at[mine8], send_sem=bsem.at[dr], recv_sem=brsem.at[dr],
-            device_id=(q * 2 + 1 - core,), device_id_type=pl.DeviceIdType.MESH,
-        ))
-    for c in [gathers[2, dr] for dr in range(16)] + both + [c for (dz, _), c in gathers.items() if dz != 2]:
+    for c in gathers.values():
         c.start()
     last = []
     for dz in (0, 1, 3, 2):
         for dr in range(16):
             if dz + dr > 0:
                 gathers[dz, dr].wait()
-        if dz == 2:
-            continue
         plane = pl.ds(pl.multiple_of(core * 512 + lax.rem(cz - dz + 4, 4) * 128, 128), 128)
         last.append(copy(out_ref.at[plane], out_ref.at[plane], twin))
     small_ref[...] = sml[...]
     small_ref[24:32, :] = sml[24:32, :] / count
-    for c in both + last:
+    for c in last:
         c.wait()
 
 
@@ -451,7 +444,6 @@
             V((HALO, NODES), BF16), V((HALO, NODES), BF16),
             pltpu.SemaphoreType.DMA((n_sem,)), pltpu.SemaphoreType.DMA((n_sem,)),
             *[pltpu.SemaphoreType.DMA((CHIPS - 1,))] * 4,
-            *[pltpu.SemaphoreType.DMA((16,))] * 2,
         ],
         name="step",
         compiler_params=pltpu.CompilerParams(

time: 82.8 us -> 82.3 us (level)
  no operation moved by 1% of the time
where the time goes in v8:
time: 82.3 us; the launch traced here: 82.2 us
  Pallas kernels  81.2 us (99%)
  between operations  0.9 us (1%)
    pallas_call x1, Pallas kernels, step(): pl.pallas_call(step_kernel, out_shape=[jax.ShapeDtypeStruct((1024, HID),...  62.3 us
    pallas_call x1, Pallas kernels, build(): pl.pallas_call(build_kernel, out_shape=[o] * 2, in_specs=[H] * 3, out_spe...  17.6 us

profile of v8, /device:TPU:1, one launch (start us, length us, event | category | flops | bytes accessed | tf_op | source)
XLA Modules:
  0.0 82.2 jit_solution(980444764948493923)
XLA Ops:
  0.6 0.0 copy-start
  0.6 0.0 copy-start.1
  0.7 0.0 copy-start.2
  0.7 0.0 copy-start.3
  0.7 0.0 copy-start.4
  0.7 0.0 copy-start.5
  0.7 17.6 %build.1 = (f32[16392,128]{1,0:T(8,128)S(1)}, f32[16392,128]{1,0:T(8,128)S(1)}) custom-call(s32[128,128]{1,0:T(8,128)} %bitcast.11, s32[128,128]{1,0:T(8,128)} %bitcast.12, f32[128,128]{1,0:T(8,128)} %bitcast.13), custom_call_target="tpu_custom_call" | custom-call | flops 10000000000 | bytes 80000000 | tf_op jit(solution)/shard_map/build/pallas_call | solution.py:139
  18.3 0.0 copy-done
  18.3 0.0 copy-done.1
  18.4 0.0 copy-done.2
  18.4 0.0 copy-done.3
  18.4 0.0 copy-done.4
  18.4 0.0 copy-done.5
  18.4 62.3 %step.1 = (f32[1024,128]{1,0:T(8,128)S(1)}, f32[32,128]{1,0:T(8,128)S(1)}) custom-call(bf16[1024,1024]{1,0:T(8,128)(2,1)S(1)} %copy-done, f32[1024,128]{1,0:T(8,128)S(1)} %copy-done.1, f32[19,128]{1,0:T(8,128)S(1)} %bitcast.8, s32[2,512]{1,0:T(2,128)S(1)} %copy-done.3, f32[16392,128]{1,0:T(8,128)S(1)} %get-tuple-element.10.ma_ref, ...), custom_call_target="tpu_custom_call" | custom-call | tf_op jit(solution)/shard_map/step/pallas_call | solution.py:424
  80.7 1.3 %finish.1 = (f32[1,1]{1,0:T(1,128)}, f32[1024,128]{1,0:T(8,128)}, f32[19,128]{1,0:T(8,128)}) custom-call(f32[1024,128]{1,0:T(8,128)S(1)} %get-tuple-element.12.one_in, f32[32,128]{1,0:T(8,128)S(1)} %get-tuple-element.13.small_in), custom_call_target="tpu_custom_call" | custom-call | tf_op jit(solution)/shard_map/finish/pallas_call | solution.py:406
Async XLA Ops:
  0.6 17.7 %copy-start = (bf16[1024,1024]{1,0:T(8,128)(2,1)S(1)}, bf16[1024,1024]{1,0:T(8,128)(2,1)}, u32[]{:S(2)}) copy-start(bf16[1024,1024]{1,0:T(8,128)(2,1)} %x_ref.1) | copy-start | bytes 6291460
  0.6 17.7 %copy-start.1 = (f32[1024,128]{1,0:T(8,128)S(1)}, f32[1024,128]{1,0:T(8,128)}, u32[]{:S(2)}) copy-start(f32[1024,128]{1,0:T(8,128)} %w1_ref.1) | copy-start | bytes 1572868
  0.7 17.7 %copy-start.2 = (f32[128,19]{0,1:T(8,128)S(1)}, f32[128,19]{0,1:T(8,128)}, u32[]{:S(2)}) copy-start(f32[128,19]{0,1:T(8,128)} %param.11) | copy-start | bytes 29188
  0.7 17.7 %copy-start.3 = (s32[2,512]{1,0:T(2,128)S(1)}, s32[2,512]{1,0:T(2,128)}, u32[]{:S(2)}) copy-start(s32[2,512]{1,0:T(2,128)} %send_ref.1) | copy-start | bytes 12292
  0.7 17.7 %copy-start.4 = (s32[1024]{0:T(1024)S(1)}, s32[1024]{0:T(1024)}, u32[]{:S(2)}) copy-start(s32[1024]{0:T(1024)} %param.16) | copy-start | bytes 12292
  0.7 17.7 %copy-start.5 = (s32[1024]{0:T(1024)S(1)}, s32[1024]{0:T(1024)}, u32[]{:S(2)}) copy-start(s32[1024]{0:T(1024)} %param.17) | copy-start | bytes 12292
